TPU v7x, 32 devices: a whole 2x2x4 slice. The times are simulated.
32 devices in a mesh: row: 4 (over y, core), phi: 8 (over z, x).
Axes of the slice: x: 2, y: 2, z: 4, core: 2. Of those that a mesh axis runs over, the one named last changes fastest.
Arguments:
- hydro_vars: float32 [5, 128, 128, 256], P(None, 'row', 'phi'), may hold values from -6 to 6
- face_b: float32 [3, 128, 128, 256], P(None, 'row', 'phi'), may hold values from -6 to 6
- widths: int32 [16], replicated, may hold values from 2 to 128, as said below
- diffusion: float32 [5, 256], replicated, may hold values from 0.01 to 0.06
Outputs:
- conserved: float32 [8, 128, 128, 256], P(None, 'row', 'phi')
- faces_out: float32 [3, 128, 128, 256], P(None, 'row', 'phi')
Inputs may be any that keep to these rules, and one draw needn't show every extreme that they name: `widths`: every width is a power of two that divides 128; the two cycles next to the poles (entries 0 and 15) use 128.
All inputs are finite; a program needn't handle non-finite values.
Results may differ from a plain program's by a relative error of at most 0.0001.
Values sent between devices are 32-bit elements; how exact they have to be, the bound alone decides.
A program may use at most 64 MiB of HBM per device.

v0:
```python
import functools

import jax
import jax.numpy as jnp
from jax import lax
from jax.experimental import pallas as pl
from jax.experimental.pallas import tpu as pltpu
from jax.sharding import PartitionSpec as P

MESH = pl.DeviceIdType.MESH
LANES = 128
SUB = 8
EARLY = 2
LIMIT = 58000000


def kernel(
    nrow, nphi, rows, cells, tiles, cycles,
    widths_far, hydro, face, diffusion_far, O, F,
    H, SL, SR, PL, PR, SF, RF, FN, Q, M, MG, ELO, EHI, EL, ER,
    widths, diffusion, small_sem, load_sem, send_phi, recv_phi, send_mean, recv_mean, send_row, recv_row,
):
    nvar = hydro.shape[0]
    nface = face.shape[0]
    fields = nvar + nface
    last = tiles - 1
    blocks = cells // SUB
    ring = cells * tiles
    row = lax.axis_index("row")
    phi = lax.axis_index("phi")
    left = lax.rem(phi + nphi - 1, nphi)
    right = lax.rem(phi + 1, nphi)
    packed = 2 * cycles

    loads = [pltpu.make_async_copy(hydro.at[k], H.at[k, pl.ds(2 * ring, rows * ring)], load_sem.at[k]) for k in range(nvar)]
    loads += [pltpu.make_async_copy(face.at[k], F.at[k], load_sem.at[nvar + k]) for k in range(nface)]
    small = [
        pltpu.make_async_copy(widths_far, widths, small_sem.at[0]),
        pltpu.make_async_copy(diffusion_far, diffusion, small_sem.at[1]),
    ]
    for c in small + loads:
        c.start()

    barrier = pltpu.get_barrier_semaphore()
    for step in range(1, nphi):
        pl.semaphore_signal(barrier, inc=1, device_id={"phi": lax.rem(phi + step, nphi)}, device_id_type=MESH)

    @pl.when(row > 0)
    def _():
        pl.semaphore_signal(barrier, inc=1, device_id={"row": row - 1}, device_id_type=MESH)

    @pl.when(row < nrow - 1)
    def _():
        pl.semaphore_signal(barrier, inc=1, device_id={"row": row + 1}, device_id_type=MESH)

    for c in small:
        c.wait()
    lane = lax.broadcasted_iota(jnp.int32, (1, LANES), 1)
    width = jnp.zeros((1, LANES), jnp.int32)
    slot = lax.rem(lane, packed)
    for j in range(cycles):
        width = jnp.where(slot == cycles + j, widths[j], width)
        width = jnp.where(slot == j, widths[cycles + j], width)
    low = lane < cycles
    high = lane >= LANES - cycles
    mine = [(lane >= packed * f) & (lane < packed * (f + 1)) for f in range(fields)]

    def part(t):
        return slice(t * LANES, (t + 1) * LANES)

    def pack(value, f):
        return pltpu.roll(value, (cycles + packed * f) % LANES, 1)

    def unpack(value, f):
        return pltpu.roll(value, (-(cycles + packed * f)) % LANES, 1)

    def spot(r, b, t):
        start = r * ring + (b * tiles + t) * SUB
        return pl.ds(start if isinstance(r, int) else pl.multiple_of(start, SUB), SUB)

    def layer(r, cell, t):
        return pl.ds(r * ring + (cell // SUB * tiles + t) * SUB + cell % SUB, rows, stride=ring)

    def place(f):
        return (H, f, 2) if f < nvar else (F, f - nvar, 0)

    def phi_copies(k):
        return (
            pltpu.make_async_remote_copy(
                src_ref=SL.at[k], dst_ref=PR.at[k], send_sem=send_phi.at[0, k], recv_sem=recv_phi.at[0, k],
                device_id={"phi": left}, device_id_type=MESH),
            pltpu.make_async_remote_copy(
                src_ref=SR.at[k], dst_ref=PL.at[k], send_sem=send_phi.at[1, k], recv_sem=recv_phi.at[1, k],
                device_id={"phi": right}, device_id_type=MESH),
        )

    def mean_copy(step):
        return pltpu.make_async_remote_copy(
            src_ref=M, dst_ref=MG.at[phi], send_sem=send_mean.at[step], recv_sem=recv_mean.at[step],
            device_id={"phi": lax.rem(phi + step, nphi)}, device_id_type=MESH)

    def pack_halo(k):
        for t in range(tiles):
            for i in range(2):
                SL[k, i, t] = H[k, layer(2, i, t), :]
                SR[k, i, t] = H[k, layer(2, cells - 2 + i, t), :]

    for c in loads:
        c.wait()

    def polar_cells(r, b):
        value = jnp.zeros((SUB, LANES), jnp.float32)
        for f in range(fields):
            ref, k, base = place(f)
            polar = jnp.where(low, ref[k, spot(r + base, b, 0), :], ref[k, spot(r + base, b, last), :])
            value = jnp.where(mine[f], pack(polar, f), value)
        return value

    def cell_mean(r, carry):
        value = jnp.zeros((SUB, LANES), jnp.float32)
        for f in range(fields):
            ref, k, base = place(f)
            sums = [ref[k, spot(r + base, 0, t), :] for t in (0, last)]
            for b in range(1, blocks):
                sums = [x + ref[k, spot(r + base, b, t), :] for x, t in zip(sums, (0, last))]
            value = jnp.where(mine[f], pack(jnp.where(low, sums[0], sums[1]), f), value)
        size = SUB // 2
        while size:
            value = value + pltpu.roll(value, size, 0)
            size //= 2
        M[pl.ds(r, 1), :] = value[0:1] * (1.0 / cells)
        return carry

    lax.fori_loop(0, rows, cell_mean, 0, unroll=4)
    peers = nphi - 1 + jnp.where(row > 0, 1, 0) + jnp.where(row < nrow - 1, 1, 0)
    pl.semaphore_wait(barrier, peers)
    for step in range(1, nphi):
        mean_copy(step).start()
    for k in range(EARLY):
        pack_halo(k)
        for c in phi_copies(k):
            c.start()

    index = lax.broadcasted_iota(jnp.int32, (SUB, LANES), 0)

    def local_average(r, carry):
        totals = [polar_cells(r, b) for b in range(blocks)]
        results = list(totals)
        size = 1
        while size < cells:
            if size < SUB:
                turned = []
                for v in totals:
                    forward = pltpu.roll(v, SUB - size, 0)
                    if 2 * size < SUB:
                        forward = jnp.where((index & size) == 0, forward, pltpu.roll(v, size, 0))
                    turned.append(v + forward)
                totals = turned
            else:
                hop = size // SUB
                totals = [totals[b] + totals[b ^ hop] for b in range(blocks)]
            size *= 2
            results = [jnp.where(width == size, v * (1.0 / size), old) for v, old in zip(totals, results)]
        for b in range(blocks):
            Q[pl.ds(pl.multiple_of(r * cells + b * SUB, SUB), SUB), :] = results[b]
        ELO[pl.ds(r, 1), :] = results[0][0:1]
        EHI[pl.ds(r, 1), :] = results[blocks - 1][SUB - 1 : SUB]
        return carry

    lax.fori_loop(0, rows, local_average, 0, unroll=2)

    edge_left = pltpu.make_async_remote_copy(
        src_ref=ELO, dst_ref=ER, send_sem=send_phi.at[0, nvar], recv_sem=recv_phi.at[0, nvar],
        device_id={"phi": left}, device_id_type=MESH)
    edge_right = pltpu.make_async_remote_copy(
        src_ref=EHI, dst_ref=EL, send_sem=send_phi.at[1, nvar], recv_sem=recv_phi.at[1, nvar],
        device_id={"phi": right}, device_id_type=MESH)
    face_left = pltpu.make_async_remote_copy(
        src_ref=SF, dst_ref=RF, send_sem=send_phi.at[0, nvar + 1], recv_sem=recv_phi.at[0, nvar + 1],
        device_id={"phi": left}, device_id_type=MESH)
    edge_left.start()
    edge_right.start()
    for t in range(tiles):
        SF[t] = F[nface - 1, layer(0, 0, t), :]
    for k in range(EARLY, nvar):
        pack_halo(k)
    for k in range(EARLY, nvar):
        for c in phi_copies(k):
            c.start()
    face_left.start()

    MG[phi] = M[...]
    for step in range(1, nphi):
        mean_copy(step).wait_recv()

    def group_mean(who, initial):
        result = initial
        size = 2
        while size <= nphi:
            start = (who // size) * size
            total = MG[start]
            for i in range(1, size):
                total = total + MG[start + i]
            result = jnp.where(width == size * cells, total * (1.0 / size), result)
            size *= 2
        return result

    own_mean = group_mean(phi, M[...])
    next_lo = group_mean(right, jnp.zeros_like(own_mean))
    next_hi = group_mean(left, jnp.zeros_like(own_mean))
    MG[phi] = own_mean
    wide = width > cells

    def spread(r):
        mean = jnp.broadcast_to(MG[phi, pl.ds(r, 1), :], (SUB, LANES))
        for b in range(blocks):
            where = pl.ds(r * cells + b * SUB if isinstance(r, int) else pl.multiple_of(r * cells + b * SUB, SUB), SUB)
            value = jnp.where(wide, mean, Q[where, :])
            for f in range(fields):
                ref, k, base = place(f)
                polar = unpack(value, f)
                ref[k, spot(r + base, b, 0), :] = jnp.where(low, polar, ref[k, spot(r + base, b, 0), :])
                ref[k, spot(r + base, b, last), :] = jnp.where(high, polar, ref[k, spot(r + base, b, last), :])

    for r in (0, 1, rows - 2, rows - 1):
        spread(r)
    lax.fori_loop(2, rows - 2, lambda r, c: (spread(r), c)[1], 0, unroll=4)

    down = pltpu.make_async_remote_copy(
        src_ref=H.at[:, pl.ds(2 * ring, 2 * ring)], dst_ref=H.at[:, pl.ds((rows + 2) * ring, 2 * ring)],
        send_sem=send_row.at[0], recv_sem=recv_row.at[0], device_id={"row": row - 1}, device_id_type=MESH)
    down_face = pltpu.make_async_remote_copy(
        src_ref=F.at[0, pl.ds(0, ring)], dst_ref=FN,
        send_sem=send_row.at[1], recv_sem=recv_row.at[1], device_id={"row": row - 1}, device_id_type=MESH)
    up = pltpu.make_async_remote_copy(
        src_ref=H.at[:, pl.ds(rows * ring, 2 * ring)], dst_ref=H.at[:, pl.ds(0, 2 * ring)],
        send_sem=send_row.at[2], recv_sem=recv_row.at[2], device_id={"row": row + 1}, device_id_type=MESH)

    @pl.when(row > 0)
    def _():
        down.start()
        down_face.start()

    @pl.when(row < nrow - 1)
    def _():
        up.start()

    @pl.when(row == 0)
    def _():
        H[:, pl.ds(0, 2 * ring), :] = jnp.zeros((nvar, 2 * ring, LANES), jnp.float32)

    @pl.when(row == nrow - 1)
    def _():
        H[:, pl.ds((rows + 2) * ring, 2 * ring), :] = jnp.zeros((nvar, 2 * ring, LANES), jnp.float32)
        FN[...] = jnp.zeros_like(FN)

    def whole(ref, k, r, t):
        return jnp.concatenate([ref[k, spot(r, b, t), :] for b in range(blocks)], 0)

    def write(k, r, t, value):
        for b in range(blocks):
            O[k, spot(r, b, t), :] = value[b * SUB : (b + 1) * SUB]

    def shifted(parts, amount):
        out = []
        turned = [pltpu.roll(p, (-amount) % LANES, 1) for p in parts]
        for t in range(tiles):
            if amount > 0:
                inside = lane < LANES - amount
                other = turned[t + 1] if t + 1 < tiles else 0.0
            else:
                inside = lane >= -amount
                other = turned[t - 1] if t > 0 else 0.0
            out.append(jnp.where(inside, turned[t], other))
        return out

    def smooth_row(r):
        for k in range(nvar):
            mid = [whole(H, k, r + 2, t) for t in range(tiles)]
            one = [a + b for a, b in zip(shifted(mid, 1), shifted(mid, -1))]
            two = [a + b for a, b in zip(shifted(mid, 2), shifted(mid, -2))]
            for t in range(tiles):
                v = mid[t]
                s1 = one[t] + (pltpu.roll(v, 1, 0) + pltpu.roll(v, cells - 1, 0)) + (whole(H, k, r + 1, t) + whole(H, k, r + 3, t))
                s2 = two[t] + (pltpu.roll(v, 2, 0) + pltpu.roll(v, cells - 2, 0)) + (whole(H, k, r, t) + whole(H, k, r + 4, t))
                change = (16.0 * s1 - s2 - 90.0 * v) * (1.0 / 12.0)
                write(k, r, t, v + diffusion[k : k + 1, part(t)] * change)

    def field_row(r, following):
        polar = [whole(F, 1, r, t) for t in range(tiles)]
        polar_next = shifted(polar, 1)
        for t in range(tiles):
            write(nvar, r, t, 0.5 * (whole(F, 0, r, t) + following(t)))
            write(nvar + 1, r, t, 0.5 * (polar[t] + polar_next[t]))
            azimuth = whole(F, 2, r, t)
            write(nvar + 2, r, t, 0.5 * (azimuth + pltpu.roll(azimuth, cells - 1, 0)))

    def inner_row(r, carry):
        field_row(r, lambda t: whole(F, 0, r + 1, t))
        smooth_row(r)
        return carry

    lax.fori_loop(2, rows - 2, inner_row, 0, unroll=2)
    for r in (0, 1, rows - 2):
        field_row(r, lambda t, r=r: whole(F, 0, r + 1, t))

    @pl.when(row > 0)
    def _():
        up.wait_recv()

    @pl.when(row < nrow - 1)
    def _():
        down.wait_recv()
        down_face.wait_recv()

    field_row(rows - 1, lambda t: jnp.concatenate([FN[spot(0, b, t), :] for b in range(blocks)], 0))
    for r in (0, 1, rows - 2, rows - 1):
        smooth_row(r)

    edge_left.wait_recv()
    edge_right.wait_recv()
    local = width <= cells
    from_left = jnp.where(local, EL[...], next_hi)
    from_right = jnp.where(local, ER[...], next_lo)

    def fixed(raw, edge, t):
        if t == 0:
            raw = jnp.where(low, edge, raw)
        if t == last:
            raw = jnp.where(high, edge, raw)
        return raw

    for k in range(nvar):
        for c in phi_copies(k):
            c.wait_recv()
        edge_l = unpack(from_left, k)
        edge_r = unpack(from_right, k)
        for t in range(tiles):
            scale = diffusion[k : k + 1, part(t)] * (1.0 / 12.0)
            l1 = fixed(PL[k, 1, t], edge_l, t) - H[k, layer(2, cells - 1, t), :]
            l2 = fixed(PL[k, 0, t], edge_l, t) - H[k, layer(2, cells - 2, t), :]
            r1 = fixed(PR[k, 0, t], edge_r, t) - H[k, layer(2, 0, t), :]
            r2 = fixed(PR[k, 1, t], edge_r, t) - H[k, layer(2, 1, t), :]
            for cell, term in ((0, 16.0 * l1 - l2), (1, -l1), (cells - 2, -r1), (cells - 1, 16.0 * r1 - r2)):
                O[k, layer(0, cell, t), :] = O[k, layer(0, cell, t), :] + scale * term

    face_left.wait_recv()
    edge_f = unpack(from_right, fields - 1)
    for t in range(tiles):
        O[fields - 1, layer(0, cells - 1, t), :] = 0.5 * (F[nface - 1, layer(0, cells - 1, t), :] + fixed(RF[t], edge_f, t))

    for k in range(nvar):
        for c in phi_copies(k):
            c.wait_send()
    edge_left.wait_send()
    edge_right.wait_send()
    face_left.wait_send()
    for step in range(1, nphi):
        mean_copy(step).wait_send()

    @pl.when(row > 0)
    def _():
        down.wait_send()
        down_face.wait_send()

    @pl.when(row < nrow - 1)
    def _():
        up.wait_send()


def spill(pieces, conserved, faces, conserved_out, faces_out, sem):
    fields = conserved.shape[0]
    size = conserved.shape[1] // pieces
    copies = []
    for k in range(fields + faces.shape[0]):
        source, target, i = (conserved, conserved_out, k) if k < fields else (faces, faces_out, k - fields)
        for p in range(pieces):
            where = pl.ds(p * size, size)
            copies.append(pltpu.make_async_copy(source.at[i, where], target.at[i, where], sem.at[k, p]))
    for c in copies:
        c.start()
    for c in copies:
        c.wait()


def blocked(x):
    n, rows, cells, theta = x.shape
    x = x.reshape(n, rows, cells // SUB, SUB, theta // LANES, LANES)
    return x.transpose(0, 1, 2, 4, 3, 5).reshape(n, rows * cells * (theta // LANES), LANES)


def unblocked(x, rows, cells, theta):
    x = x.reshape(x.shape[0], rows, cells // SUB, theta // LANES, SUB, LANES)
    return x.transpose(0, 1, 2, 4, 3, 5).reshape(x.shape[0], rows, cells, theta)


def body(nrow, nphi, hydro_vars, face_b, widths, diffusion):
    nvar, rows, cells, theta = hydro_vars.shape
    nface = face_b.shape[0]
    fields = nvar + nface
    cycles = widths.shape[0] // 2
    tiles = theta // LANES
    ring = cells * tiles
    f32 = jnp.float32
    shape = lambda *s: pltpu.VMEM(s, f32)
    far = pl.BlockSpec(memory_space=pltpu.HBM)
    near = pl.BlockSpec(memory_space=pltpu.VMEM)
    result_bytes = (fields + nface) * rows * ring * LANES * 4
    conserved, faces = pl.pallas_call(
        functools.partial(kernel, nrow, nphi, rows, cells, tiles, cycles),
        out_shape=(
            pltpu.VMEM((fields, rows * ring, LANES), f32),
            pltpu.VMEM((nface, rows * ring, LANES), f32),
        ),
        in_specs=[far, far, far, far],
        out_specs=(near, near),
        scratch_shapes=[
            shape(nvar, (rows + 4) * ring, LANES),
            shape(nvar, 2, tiles, rows, LANES),
            shape(nvar, 2, tiles, rows, LANES),
            shape(nvar, 2, tiles, rows, LANES),
            shape(nvar, 2, tiles, rows, LANES),
            shape(tiles, rows, LANES),
            shape(tiles, rows, LANES),
            shape(ring, LANES),
            shape(rows * cells, LANES),
            shape(rows, LANES),
            shape(nphi, rows, LANES),
            shape(rows, LANES),
            shape(rows, LANES),
            shape(rows, LANES),
            shape(rows, LANES),
            pltpu.SMEM((2 * cycles,), jnp.int32),
            shape(nvar, theta),
            pltpu.SemaphoreType.DMA((2,)),
            pltpu.SemaphoreType.DMA((fields,)),
            pltpu.SemaphoreType.DMA((2, nvar + 2)),
            pltpu.SemaphoreType.DMA((2, nvar + 2)),
            pltpu.SemaphoreType.DMA((nphi,)),
            pltpu.SemaphoreType.DMA((nphi,)),
            pltpu.SemaphoreType.DMA((3,)),
            pltpu.SemaphoreType.DMA((3,)),
        ],
        compiler_params=pltpu.CompilerParams(
            collective_id=0, has_side_effects=True, vmem_limit_bytes=LIMIT - result_bytes
        ),
        name="step",
    )(widths, blocked(hydro_vars), blocked(face_b), diffusion)
    pieces = 2
    conserved, faces = pl.pallas_call(
        functools.partial(spill, pieces),
        out_shape=(
            jax.ShapeDtypeStruct((fields, rows * ring, LANES), f32),
            jax.ShapeDtypeStruct((nface, rows * ring, LANES), f32),
        ),
        in_specs=[near, near],
        out_specs=(far, far),
        scratch_shapes=[pltpu.SemaphoreType.DMA((fields + nface, pieces))],
        compiler_params=pltpu.CompilerParams(vmem_limit_bytes=1000000),
        name="spill",
    )(conserved, faces)
    return unblocked(conserved, rows, cells, theta), unblocked(faces, rows, cells, theta)


def solution(mesh):
    spec = P(None, "row", "phi", None)
    return jax.shard_map(
        functools.partial(body, mesh.shape["row"], mesh.shape["phi"]),
        mesh=mesh,
        in_specs=(spec, spec, P(), P()),
        out_specs=(spec, spec),
        check_vma=False,
    )
```

profile of v0, /device:TPU:0, one launch (start us, length us, event | category | flops | bytes accessed | tf_op | source)
XLA Modules:
  0.0 27.8 jit_solution(5934905198295485429)
XLA Ops:
  0.6 24.5 %step.1 = (f32[8,1024,128]{2,1,0:T(8,128)S(1)}, f32[3,1024,128]{2,1,0:T(8,128)S(1)}) custom-call(s32[16]{0:T(128)} %widths_far.1, f32[5,1024,128]{2,1,0:T(8,128)} %bitcast.20, f32[3,1024,128]{2,1,0:T(8,128)} %bitcast.21, f32[5,256]{1,0:T(8,128)} %diffusion_far.1), custom_call_target="tpu_custom_call" | custom-call | tf_op jit(solution)/shard_map/step/pallas_call | solution.py:409
  25.2 2.7 %spill.1 = (f32[8,1024,128]{2,1,0:T(8,128)}, f32[3,1024,128]{2,1,0:T(8,128)}) custom-call(f32[8,1024,128]{2,1,0:T(8,128)S(1)} %get-tuple-element.6.conserved, f32[3,1024,128]{2,1,0:T(8,128)S(1)} %get-tuple-element.7.faces), custom_call_target="tpu_custom_call" | custom-call | tf_op jit(solution)/shard_map/spill/pallas_call | solution.py:450
where the time goes:
time: 28 us; the launch traced here: 27.8 us
  Pallas kernels  27.2 us (97%)
  between operations  0.64 us (2%)
    pallas_call x1, Pallas kernels, body(): pl.pallas_call(functools.partial(kernel, nrow, nphi, rows, cells, tiles,...  24.5 us
    pallas_call x1, Pallas kernels, body(): pl.pallas_call(functools.partial(spill, pieces), out_shape=(jax.ShapeDtyp...  2.67 us

commit v1 on v0

--- a/solution.py
+++ b/solution.py
@@ -17,8 +17,9 @@
 def kernel(
     nrow, nphi, rows, cells, tiles, cycles,
     widths_far, hydro, face, diffusion_far, O, F,
-    H, SL, SR, PL, PR, SF, RF, FN, Q, M, MG, ELO, EHI, EL, ER,
-    widths, diffusion, small_sem, load_sem, send_phi, recv_phi, send_mean, recv_mean, send_row, recv_row,
+    H, S, R, SF, RF, FN, Q, M, PX, OM, MG, ELO, EHI, EL, ER,
+    widths, diffusion, small_sem, load_sem, send_phi, recv_phi, send_edge, recv_edge,
+    send_mean, recv_mean, send_row, recv_row, pair_ack, wrap_ack,
 ):
     nvar = hydro.shape[0]
     nface = face.shape[0]
@@ -30,6 +31,12 @@
     phi = lax.axis_index("phi")
     left = lax.rem(phi + nphi - 1, nphi)
     right = lax.rem(phi + 1, nphi)
+    pairs = nphi // 2
+    pair = phi // 2
+    odd = lax.rem(phi, 2)
+    partner = phi + 1 - 2 * odd
+    far = jnp.where(odd == 1, right, left)
+    near_way, far_way = 1 - odd, odd
     packed = 2 * cycles
 
     loads = [pltpu.make_async_copy(hydro.at[k], H.at[k, pl.ds(2 * ring, rows * ring)], load_sem.at[k]) for k in range(nvar)]
@@ -42,25 +49,31 @@
         c.start()
 
     barrier = pltpu.get_barrier_semaphore()
-    for step in range(1, nphi):
-        pl.semaphore_signal(barrier, inc=1, device_id={"phi": lax.rem(phi + step, nphi)}, device_id_type=MESH)
+
+    def greet(**device):
+        pl.semaphore_signal(barrier, inc=1, device_id=device, device_id_type=MESH)
+
+    greet(phi=partner)
+
+    @pl.when(phi < nphi - 1)
+    def _():
+        greet(phi=far)
 
     @pl.when(row > 0)
     def _():
-        pl.semaphore_signal(barrier, inc=1, device_id={"row": row - 1}, device_id_type=MESH)
+        greet(row=row - 1)
 
     @pl.when(row < nrow - 1)
     def _():
-        pl.semaphore_signal(barrier, inc=1, device_id={"row": row + 1}, device_id_type=MESH)
-
-    for c in small:
-        c.wait()
+        greet(row=row + 1)
+
+    for step in range(1, pairs):
+
+        @pl.when(pair + step < pairs)
+        def _(step=step):
+            greet(phi=phi + 2 * step)
+
     lane = lax.broadcasted_iota(jnp.int32, (1, LANES), 1)
-    width = jnp.zeros((1, LANES), jnp.int32)
-    slot = lax.rem(lane, packed)
-    for j in range(cycles):
-        width = jnp.where(slot == cycles + j, widths[j], width)
-        width = jnp.where(slot == j, widths[cycles + j], width)
     low = lane < cycles
     high = lane >= LANES - cycles
     mine = [(lane >= packed * f) & (lane < packed * (f + 1)) for f in range(fields)]
@@ -84,28 +97,52 @@
     def place(f):
         return (H, f, 2) if f < nvar else (F, f - nvar, 0)
 
-    def phi_copies(k):
-        return (
-            pltpu.make_async_remote_copy(
-                src_ref=SL.at[k], dst_ref=PR.at[k], send_sem=send_phi.at[0, k], recv_sem=recv_phi.at[0, k],
-                device_id={"phi": left}, device_id_type=MESH),
-            pltpu.make_async_remote_copy(
-                src_ref=SR.at[k], dst_ref=PL.at[k], send_sem=send_phi.at[1, k], recv_sem=recv_phi.at[1, k],
-                device_id={"phi": right}, device_id_type=MESH),
-        )
+    def halo(way, target, k):
+        return pltpu.make_async_remote_copy(
+            src_ref=S.at[way, k], dst_ref=R.at[way, k], send_sem=send_phi.at[way, k], recv_sem=recv_phi.at[way, k],
+            device_id={"phi": target}, device_id_type=MESH)
+
+    def near_copy(k):
+        return halo(near_way, partner, k)
+
+    def far_copy(k):
+        return halo(far_way, far, k)
+
+    mean_near = pltpu.make_async_remote_copy(
+        src_ref=M, dst_ref=PX, send_sem=send_mean.at[0], recv_sem=recv_mean.at[0],
+        device_id={"phi": partner}, device_id_type=MESH)
 
     def mean_copy(step):
         return pltpu.make_async_remote_copy(
-            src_ref=M, dst_ref=MG.at[phi], send_sem=send_mean.at[step], recv_sem=recv_mean.at[step],
-            device_id={"phi": lax.rem(phi + step, nphi)}, device_id_type=MESH)
+            src_ref=MG.at[pair], dst_ref=MG.at[pair], send_sem=send_mean.at[step], recv_sem=recv_mean.at[step],
+            device_id={"phi": lax.rem(phi + 2 * step, nphi)}, device_id_type=MESH)
 
     def pack_halo(k):
         for t in range(tiles):
             for i in range(2):
-                SL[k, i, t] = H[k, layer(2, i, t), :]
-                SR[k, i, t] = H[k, layer(2, cells - 2 + i, t), :]
-
-    for c in loads:
+                S[0, k, i, t] = H[k, layer(2, i, t), :]
+                S[1, k, i, t] = H[k, layer(2, cells - 2 + i, t), :]
+
+    for k in range(nvar):
+        loads[k].wait()
+        pack_halo(k)
+        if k == 0:
+            known = 1 + jnp.where(phi > 0, 1, 0) + pair
+            known = known + jnp.where(row > 0, 1, 0) + jnp.where(row < nrow - 1, 1, 0)
+            pl.semaphore_wait(barrier, known)
+            for step in range(1, pairs):
+
+                @pl.when(pair >= step)
+                def _(step=step):
+                    pl.semaphore_signal(pair_ack.at[step], inc=1, device_id={"phi": phi - 2 * step}, device_id_type=MESH)
+
+            @pl.when(phi == nphi - 1)
+            def _():
+                pl.semaphore_signal(wrap_ack, inc=1, device_id={"phi": 0}, device_id_type=MESH)
+
+        if k < EARLY:
+            near_copy(k).start()
+    for c in loads[nvar:]:
         c.wait()
 
     def polar_cells(r, b):
@@ -132,14 +169,25 @@
         return carry
 
     lax.fori_loop(0, rows, cell_mean, 0, unroll=4)
-    peers = nphi - 1 + jnp.where(row > 0, 1, 0) + jnp.where(row < nrow - 1, 1, 0)
-    pl.semaphore_wait(barrier, peers)
-    for step in range(1, nphi):
-        mean_copy(step).start()
-    for k in range(EARLY):
-        pack_halo(k)
-        for c in phi_copies(k):
-            c.start()
+    mean_near.start()
+
+    @pl.when(phi > 0)
+    def _():
+        for k in range(EARLY):
+            far_copy(k).start()
+
+    for k in range(EARLY, nvar):
+        near_copy(k).start()
+    for t in range(tiles):
+        SF[t] = F[nface - 1, layer(0, 0, t), :]
+
+    for c in small:
+        c.wait()
+    width = jnp.zeros((1, LANES), jnp.int32)
+    slot = lax.rem(lane, packed)
+    for j in range(cycles):
+        width = jnp.where(slot == cycles + j, widths[j], width)
+        width = jnp.where(slot == j, widths[cycles + j], width)
 
     index = lax.broadcasted_iota(jnp.int32, (SUB, LANES), 0)
 
@@ -170,49 +218,58 @@
     lax.fori_loop(0, rows, local_average, 0, unroll=2)
 
     edge_left = pltpu.make_async_remote_copy(
-        src_ref=ELO, dst_ref=ER, send_sem=send_phi.at[0, nvar], recv_sem=recv_phi.at[0, nvar],
+        src_ref=ELO, dst_ref=ER, send_sem=send_edge.at[0], recv_sem=recv_edge.at[0],
         device_id={"phi": left}, device_id_type=MESH)
     edge_right = pltpu.make_async_remote_copy(
-        src_ref=EHI, dst_ref=EL, send_sem=send_phi.at[1, nvar], recv_sem=recv_phi.at[1, nvar],
+        src_ref=EHI, dst_ref=EL, send_sem=send_edge.at[1], recv_sem=recv_edge.at[1],
         device_id={"phi": right}, device_id_type=MESH)
     face_left = pltpu.make_async_remote_copy(
-        src_ref=SF, dst_ref=RF, send_sem=send_phi.at[0, nvar + 1], recv_sem=recv_phi.at[0, nvar + 1],
+        src_ref=SF, dst_ref=RF, send_sem=send_edge.at[2], recv_sem=recv_edge.at[2],
         device_id={"phi": left}, device_id_type=MESH)
+    mean_near.wait_recv()
+    MG[pair] = (M[...] + PX[...]) * 0.5
+    for step in range(1, pairs):
+
+        @pl.when(pair + step < pairs)
+        def _(step=step):
+            pl.semaphore_wait(pair_ack.at[step], 1)
+
+        mean_copy(step).start()
+
+    @pl.when(phi == 0)
+    def _():
+        pl.semaphore_wait(wrap_ack, 1)
+        for k in range(EARLY):
+            far_copy(k).start()
+
+    for k in range(EARLY, nvar):
+        far_copy(k).start()
     edge_left.start()
     edge_right.start()
-    for t in range(tiles):
-        SF[t] = F[nface - 1, layer(0, 0, t), :]
-    for k in range(EARLY, nvar):
-        pack_halo(k)
-    for k in range(EARLY, nvar):
-        for c in phi_copies(k):
-            c.start()
     face_left.start()
 
-    MG[phi] = M[...]
-    for step in range(1, nphi):
+    for step in range(1, pairs):
         mean_copy(step).wait_recv()
 
-    def group_mean(who, initial):
-        result = initial
+    def group_mean(who):
+        result = MG[who // 2]
         size = 2
-        while size <= nphi:
-            start = (who // size) * size
+        while size <= pairs:
+            start = (who // (2 * size)) * size
             total = MG[start]
             for i in range(1, size):
                 total = total + MG[start + i]
-            result = jnp.where(width == size * cells, total * (1.0 / size), result)
+            result = jnp.where(width == 2 * size * cells, total * (1.0 / size), result)
             size *= 2
         return result
 
-    own_mean = group_mean(phi, M[...])
-    next_lo = group_mean(right, jnp.zeros_like(own_mean))
-    next_hi = group_mean(left, jnp.zeros_like(own_mean))
-    MG[phi] = own_mean
+    OM[...] = group_mean(phi)
+    next_lo = group_mean(right)
+    next_hi = group_mean(left)
     wide = width > cells
 
     def spread(r):
-        mean = jnp.broadcast_to(MG[phi, pl.ds(r, 1), :], (SUB, LANES))
+        mean = jnp.broadcast_to(OM[pl.ds(r, 1), :], (SUB, LANES))
         for b in range(blocks):
             where = pl.ds(r * cells + b * SUB if isinstance(r, int) else pl.multiple_of(r * cells + b * SUB, SUB), SUB)
             value = jnp.where(wide, mean, Q[where, :])
@@ -331,16 +388,16 @@
         return raw
 
     for k in range(nvar):
-        for c in phi_copies(k):
-            c.wait_recv()
+        halo(1, right, k).wait_recv()
+        halo(0, left, k).wait_recv()
         edge_l = unpack(from_left, k)
         edge_r = unpack(from_right, k)
         for t in range(tiles):
             scale = diffusion[k : k + 1, part(t)] * (1.0 / 12.0)
-            l1 = fixed(PL[k, 1, t], edge_l, t) - H[k, layer(2, cells - 1, t), :]
-            l2 = fixed(PL[k, 0, t], edge_l, t) - H[k, layer(2, cells - 2, t), :]
-            r1 = fixed(PR[k, 0, t], edge_r, t) - H[k, layer(2, 0, t), :]
-            r2 = fixed(PR[k, 1, t], edge_r, t) - H[k, layer(2, 1, t), :]
+            l1 = fixed(R[1, k, 1, t], edge_l, t) - H[k, layer(2, cells - 1, t), :]
+            l2 = fixed(R[1, k, 0, t], edge_l, t) - H[k, layer(2, cells - 2, t), :]
+            r1 = fixed(R[0, k, 0, t], edge_r, t) - H[k, layer(2, 0, t), :]
+            r2 = fixed(R[0, k, 1, t], edge_r, t) - H[k, layer(2, 1, t), :]
             for cell, term in ((0, 16.0 * l1 - l2), (1, -l1), (cells - 2, -r1), (cells - 1, 16.0 * r1 - r2)):
                 O[k, layer(0, cell, t), :] = O[k, layer(0, cell, t), :] + scale * term
 
@@ -350,12 +407,13 @@
         O[fields - 1, layer(0, cells - 1, t), :] = 0.5 * (F[nface - 1, layer(0, cells - 1, t), :] + fixed(RF[t], edge_f, t))
 
     for k in range(nvar):
-        for c in phi_copies(k):
-            c.wait_send()
+        near_copy(k).wait_send()
+        far_copy(k).wait_send()
     edge_left.wait_send()
     edge_right.wait_send()
     face_left.wait_send()
-    for step in range(1, nphi):
+    mean_near.wait_send()
+    for step in range(1, pairs):
         mean_copy(step).wait_send()
 
     @pl.when(row > 0)
@@ -416,16 +474,16 @@
         out_specs=(near, near),
         scratch_shapes=[
             shape(nvar, (rows + 4) * ring, LANES),
-            shape(nvar, 2, tiles, rows, LANES),
-            shape(nvar, 2, tiles, rows, LANES),
-            shape(nvar, 2, tiles, rows, LANES),
-            shape(nvar, 2, tiles, rows, LANES),
+            shape(2, nvar, 2, tiles, rows, LANES),
+            shape(2, nvar, 2, tiles, rows, LANES),
             shape(tiles, rows, LANES),
             shape(tiles, rows, LANES),
             shape(ring, LANES),
             shape(rows * cells, LANES),
             shape(rows, LANES),
-            shape(nphi, rows, LANES),
+            shape(rows, LANES),
+            shape(rows, LANES),
+            shape(nphi // 2, rows, LANES),
             shape(rows, LANES),
             shape(rows, LANES),
             shape(rows, LANES),
@@ -434,12 +492,16 @@
             shape(nvar, theta),
             pltpu.SemaphoreType.DMA((2,)),
             pltpu.SemaphoreType.DMA((fields,)),
-            pltpu.SemaphoreType.DMA((2, nvar + 2)),
-            pltpu.SemaphoreType.DMA((2, nvar + 2)),
-            pltpu.SemaphoreType.DMA((nphi,)),
-            pltpu.SemaphoreType.DMA((nphi,)),
+            pltpu.SemaphoreType.DMA((2, nvar)),
+            pltpu.SemaphoreType.DMA((2, nvar)),
             pltpu.SemaphoreType.DMA((3,)),
             pltpu.SemaphoreType.DMA((3,)),
+            pltpu.SemaphoreType.DMA((nphi // 2,)),
+            pltpu.SemaphoreType.DMA((nphi // 2,)),
+            pltpu.SemaphoreType.DMA((3,)),
+            pltpu.SemaphoreType.DMA((3,)),
+            pltpu.SemaphoreType.REGULAR((nphi // 2,)),
+            pltpu.SemaphoreType.REGULAR,
         ],
         compiler_params=pltpu.CompilerParams(
             collective_id=0, has_side_effects=True, vmem_limit_bytes=LIMIT - result_bytes

time: 28 us -> 30.6 us (1.093)
  the two profiles are of different devices: /device:TPU:0 before, /device:TPU:1 now
where the time goes in v1:
time: 30.6 us; the launch traced here: 30.4 us
  Pallas kernels  29.8 us (97%)
  between operations  0.64 us (2%)
    pallas_call x1, Pallas kernels, body(): pl.pallas_call(functools.partial(kernel, nrow, nphi, rows, cells, tiles,...  27.1 us
    pallas_call x1, Pallas kernels, body(): pl.pallas_call(functools.partial(spill, pieces), out_shape=(jax.ShapeDtyp...  2.67 us

profile of v1, /device:TPU:1, one launch (start us, length us, event | category | flops | bytes accessed | tf_op | source)
XLA Modules:
  0.0 30.4 jit_solution(585276318914718788)
XLA Ops:
  0.6 27.1 %step.1 = (f32[8,1024,128]{2,1,0:T(8,128)S(1)}, f32[3,1024,128]{2,1,0:T(8,128)S(1)}) custom-call(s32[16]{0:T(128)} %widths_far.1, f32[5,1024,128]{2,1,0:T(8,128)} %bitcast.20, f32[3,1024,128]{2,1,0:T(8,128)} %bitcast.21, f32[5,256]{1,0:T(8,128)} %diffusion_far.1), custom_call_target="tpu_custom_call" | custom-call | tf_op jit(solution)/shard_map/step/pallas_call | solution.py:467
  27.8 2.7 %spill.1 = (f32[8,1024,128]{2,1,0:T(8,128)}, f32[3,1024,128]{2,1,0:T(8,128)}) custom-call(f32[8,1024,128]{2,1,0:T(8,128)S(1)} %get-tuple-element.6.conserved, f32[3,1024,128]{2,1,0:T(8,128)S(1)} %get-tuple-element.7.faces), custom_call_target="tpu_custom_call" | custom-call | tf_op jit(solution)/shard_map/spill/pallas_call | solution.py:512

commit v2 on v1

--- a/solution.py
+++ b/solution.py
@@ -10,16 +10,17 @@
 MESH = pl.DeviceIdType.MESH
 LANES = 128
 SUB = 8
-EARLY = 2
+EARLY = 1
+MIDDLE = 2
 LIMIT = 58000000
 
 
 def kernel(
     nrow, nphi, rows, cells, tiles, cycles,
     widths_far, hydro, face, diffusion_far, O, F,
-    H, S, R, SF, RF, FN, Q, M, PX, OM, MG, ELO, EHI, EL, ER,
+    H, S, R, SF, RF, FN, Q, M, PX, OM, MG, E, EX,
     widths, diffusion, small_sem, load_sem, send_phi, recv_phi, send_edge, recv_edge,
-    send_mean, recv_mean, send_row, recv_row, pair_ack, wrap_ack,
+    send_mean, recv_mean, send_row, recv_row, pair_ack, far_ack, row_ack,
 ):
     nvar = hydro.shape[0]
     nface = face.shape[0]
@@ -55,13 +56,9 @@
 
     greet(phi=partner)
 
-    @pl.when(phi < nphi - 1)
+    @pl.when(far > phi)
     def _():
         greet(phi=far)
-
-    @pl.when(row > 0)
-    def _():
-        greet(row=row - 1)
 
     @pl.when(row < nrow - 1)
     def _():
@@ -127,8 +124,7 @@
         loads[k].wait()
         pack_halo(k)
         if k == 0:
-            known = 1 + jnp.where(phi > 0, 1, 0) + pair
-            known = known + jnp.where(row > 0, 1, 0) + jnp.where(row < nrow - 1, 1, 0)
+            known = 1 + jnp.where(far < phi, 1, 0) + pair + jnp.where(row > 0, 1, 0)
             pl.semaphore_wait(barrier, known)
             for step in range(1, pairs):
 
@@ -136,9 +132,13 @@
                 def _(step=step):
                     pl.semaphore_signal(pair_ack.at[step], inc=1, device_id={"phi": phi - 2 * step}, device_id_type=MESH)
 
-            @pl.when(phi == nphi - 1)
+            @pl.when(far < phi)
             def _():
-                pl.semaphore_signal(wrap_ack, inc=1, device_id={"phi": 0}, device_id_type=MESH)
+                pl.semaphore_signal(far_ack, inc=1, device_id={"phi": far}, device_id_type=MESH)
+
+            @pl.when(row > 0)
+            def _():
+                pl.semaphore_signal(row_ack, inc=1, device_id={"row": row - 1}, device_id_type=MESH)
 
         if k < EARLY:
             near_copy(k).start()
@@ -170,13 +170,7 @@
 
     lax.fori_loop(0, rows, cell_mean, 0, unroll=4)
     mean_near.start()
-
-    @pl.when(phi > 0)
-    def _():
-        for k in range(EARLY):
-            far_copy(k).start()
-
-    for k in range(EARLY, nvar):
+    for k in range(EARLY, MIDDLE):
         near_copy(k).start()
     for t in range(tiles):
         SF[t] = F[nface - 1, layer(0, 0, t), :]
@@ -211,21 +205,29 @@
             results = [jnp.where(width == size, v * (1.0 / size), old) for v, old in zip(totals, results)]
         for b in range(blocks):
             Q[pl.ds(pl.multiple_of(r * cells + b * SUB, SUB), SUB), :] = results[b]
-        ELO[pl.ds(r, 1), :] = results[0][0:1]
-        EHI[pl.ds(r, 1), :] = results[blocks - 1][SUB - 1 : SUB]
+        E[0, pl.ds(r, 1), :] = results[0][0:1]
+        E[1, pl.ds(r, 1), :] = results[blocks - 1][SUB - 1 : SUB]
         return carry
 
     lax.fori_loop(0, rows, local_average, 0, unroll=2)
 
-    edge_left = pltpu.make_async_remote_copy(
-        src_ref=ELO, dst_ref=ER, send_sem=send_edge.at[0], recv_sem=recv_edge.at[0],
-        device_id={"phi": left}, device_id_type=MESH)
-    edge_right = pltpu.make_async_remote_copy(
-        src_ref=EHI, dst_ref=EL, send_sem=send_edge.at[1], recv_sem=recv_edge.at[1],
-        device_id={"phi": right}, device_id_type=MESH)
+    def edge_copy(way, target):
+        return pltpu.make_async_remote_copy(
+            src_ref=E.at[way], dst_ref=EX.at[way], send_sem=send_edge.at[way], recv_sem=recv_edge.at[way],
+            device_id={"phi": target}, device_id_type=MESH)
+
     face_left = pltpu.make_async_remote_copy(
         src_ref=SF, dst_ref=RF, send_sem=send_edge.at[2], recv_sem=recv_edge.at[2],
         device_id={"phi": left}, device_id_type=MESH)
+    edge_copy(near_way, partner).start()
+
+    @pl.when(odd == 1)
+    def _():
+        face_left.start()
+
+    for k in range(MIDDLE, nvar):
+        near_copy(k).start()
+
     mean_near.wait_recv()
     MG[pair] = (M[...] + PX[...]) * 0.5
     for step in range(1, pairs):
@@ -236,17 +238,18 @@
 
         mean_copy(step).start()
 
-    @pl.when(phi == 0)
-    def _():
-        pl.semaphore_wait(wrap_ack, 1)
-        for k in range(EARLY):
-            far_copy(k).start()
-
-    for k in range(EARLY, nvar):
+    @pl.when(far > phi)
+    def _():
+        pl.semaphore_wait(far_ack, 1)
+
+    edge_copy(far_way, far).start()
+
+    @pl.when(odd == 0)
+    def _():
+        face_left.start()
+
+    for k in range(nvar):
         far_copy(k).start()
-    edge_left.start()
-    edge_right.start()
-    face_left.start()
 
     for step in range(1, pairs):
         mean_copy(step).wait_recv()
@@ -300,6 +303,7 @@
 
     @pl.when(row < nrow - 1)
     def _():
+        pl.semaphore_wait(row_ack, 1)
         up.start()
 
     @pl.when(row == 0)
@@ -374,11 +378,11 @@
     for r in (0, 1, rows - 2, rows - 1):
         smooth_row(r)
 
-    edge_left.wait_recv()
-    edge_right.wait_recv()
+    edge_copy(1, right).wait_recv()
+    edge_copy(0, left).wait_recv()
     local = width <= cells
-    from_left = jnp.where(local, EL[...], next_hi)
-    from_right = jnp.where(local, ER[...], next_lo)
+    from_left = jnp.where(local, EX[1], next_hi)
+    from_right = jnp.where(local, EX[0], next_lo)
 
     def fixed(raw, edge, t):
         if t == 0:
@@ -386,6 +390,11 @@
         if t == last:
             raw = jnp.where(high, edge, raw)
         return raw
+
+    face_left.wait_recv()
+    edge_f = unpack(from_right, fields - 1)
+    for t in range(tiles):
+        O[fields - 1, layer(0, cells - 1, t), :] = 0.5 * (F[nface - 1, layer(0, cells - 1, t), :] + fixed(RF[t], edge_f, t))
 
     for k in range(nvar):
         halo(1, right, k).wait_recv()
@@ -401,16 +410,11 @@
             for cell, term in ((0, 16.0 * l1 - l2), (1, -l1), (cells - 2, -r1), (cells - 1, 16.0 * r1 - r2)):
                 O[k, layer(0, cell, t), :] = O[k, layer(0, cell, t), :] + scale * term
 
-    face_left.wait_recv()
-    edge_f = unpack(from_right, fields - 1)
-    for t in range(tiles):
-        O[fields - 1, layer(0, cells - 1, t), :] = 0.5 * (F[nface - 1, layer(0, cells - 1, t), :] + fixed(RF[t], edge_f, t))
-
     for k in range(nvar):
         near_copy(k).wait_send()
         far_copy(k).wait_send()
-    edge_left.wait_send()
-    edge_right.wait_send()
+    edge_copy(near_way, partner).wait_send()
+    edge_copy(far_way, far).wait_send()
     face_left.wait_send()
     mean_near.wait_send()
     for step in range(1, pairs):
@@ -484,10 +488,8 @@
             shape(rows, LANES),
             shape(rows, LANES),
             shape(nphi // 2, rows, LANES),
-            shape(rows, LANES),
-            shape(rows, LANES),
-            shape(rows, LANES),
-            shape(rows, LANES),
+            shape(2, rows, LANES),
+            shape(2, rows, LANES),
             pltpu.SMEM((2 * cycles,), jnp.int32),
             shape(nvar, theta),
             pltpu.SemaphoreType.DMA((2,)),
@@ -501,6 +503,7 @@
             pltpu.SemaphoreType.DMA((3,)),
             pltpu.SemaphoreType.DMA((3,)),
             pltpu.SemaphoreType.REGULAR((nphi // 2,)),
+            pltpu.SemaphoreType.REGULAR,
             pltpu.SemaphoreType.REGULAR,
         ],
         compiler_params=pltpu.CompilerParams(

time: 30.6 us -> 27.8 us (0.908)
  the two profiles are of different devices: /device:TPU:1 before, /device:TPU:25 now
where the time goes in v2:
time: 27.8 us; the launch traced here: 27.7 us
  Pallas kernels  27 us (97%)
  between operations  0.64 us (2%)
    pallas_call x1, Pallas kernels, body(): pl.pallas_call(functools.partial(kernel, nrow, nphi, rows, cells, tiles,...  24.4 us
    pallas_call x1, Pallas kernels, body(): pl.pallas_call(functools.partial(spill, pieces), out_shape=(jax.ShapeDtyp...  2.67 us

profile of v2, /device:TPU:25, one launch (start us, length us, event | category | flops | bytes accessed | tf_op | source)
XLA Modules:
  0.0 27.7 jit_solution(17164888690581125652)
XLA Ops:
  0.6 24.4 %step.1 = (f32[8,1024,128]{2,1,0:T(8,128)S(1)}, f32[3,1024,128]{2,1,0:T(8,128)S(1)}) custom-call(s32[16]{0:T(128)} %widths_far.1, f32[5,1024,128]{2,1,0:T(8,128)} %bitcast.20, f32[3,1024,128]{2,1,0:T(8,128)} %bitcast.21, f32[5,256]{1,0:T(8,128)} %diffusion_far.1), custom_call_target="tpu_custom_call" | custom-call | tf_op jit(solution)/shard_map/step/pallas_call | solution.py:471
  25.0 2.7 %spill.1 = (f32[8,1024,128]{2,1,0:T(8,128)}, f32[3,1024,128]{2,1,0:T(8,128)}) custom-call(f32[8,1024,128]{2,1,0:T(8,128)S(1)} %get-tuple-element.6.conserved, f32[3,1024,128]{2,1,0:T(8,128)S(1)} %get-tuple-element.7.faces), custom_call_target="tpu_custom_call" | custom-call | tf_op jit(solution)/shard_map/spill/pallas_call | solution.py:515

commit v3 on v2

--- a/solution.py
+++ b/solution.py
@@ -238,21 +238,32 @@
 
         mean_copy(step).start()
 
-    @pl.when(far > phi)
-    def _():
-        pl.semaphore_wait(far_ack, 1)
-
-    edge_copy(far_way, far).start()
-
-    @pl.when(odd == 0)
-    def _():
-        face_left.start()
-
-    for k in range(nvar):
-        far_copy(k).start()
-
-    for step in range(1, pairs):
+    def start_far():
+        @pl.when(far > phi)
+        def _():
+            pl.semaphore_wait(far_ack, 1)
+
+        edge_copy(far_way, far).start()
+
+        @pl.when(odd == 0)
+        def _():
+            face_left.start()
+
+        for k in range(nvar):
+            far_copy(k).start()
+
+    @pl.when(phi > 0)
+    def _():
+        start_far()
+
+    for step in range(pairs - 1, 1, -1):
         mean_copy(step).wait_recv()
+
+    @pl.when(phi == 0)
+    def _():
+        start_far()
+
+    mean_copy(1).wait_recv()
 
     def group_mean(who):
         result = MG[who // 2]

time: 27.8 us -> 25.5 us (0.917)
  the two profiles are of different devices: /device:TPU:25 before, /device:TPU:0 now
where the time goes in v3:
time: 25.5 us; the launch traced here: 25.3 us
  Pallas kernels  24.7 us (97%)
  between operations  0.64 us (3%)
    pallas_call x1, Pallas kernels, body(): pl.pallas_call(functools.partial(kernel, nrow, nphi, rows, cells, tiles,...  22 us
    pallas_call x1, Pallas kernels, body(): pl.pallas_call(functools.partial(spill, pieces), out_shape=(jax.ShapeDtyp...  2.67 us

profile of v3, /device:TPU:0, one launch (start us, length us, event | category | flops | bytes accessed | tf_op | source)
XLA Modules:
  0.0 25.3 jit_solution(17610851168686181737)
XLA Ops:
  0.6 22.0 %step.1 = (f32[8,1024,128]{2,1,0:T(8,128)S(1)}, f32[3,1024,128]{2,1,0:T(8,128)S(1)}) custom-call(s32[16]{0:T(128)} %widths_far.1, f32[5,1024,128]{2,1,0:T(8,128)} %bitcast.20, f32[3,1024,128]{2,1,0:T(8,128)} %bitcast.21, f32[5,256]{1,0:T(8,128)} %diffusion_far.1), custom_call_target="tpu_custom_call" | custom-call | tf_op jit(solution)/shard_map/step/pallas_call | solution.py:482
  22.6 2.7 %spill.1 = (f32[8,1024,128]{2,1,0:T(8,128)}, f32[3,1024,128]{2,1,0:T(8,128)}) custom-call(f32[8,1024,128]{2,1,0:T(8,128)S(1)} %get-tuple-element.6.conserved, f32[3,1024,128]{2,1,0:T(8,128)S(1)} %get-tuple-element.7.faces), custom_call_target="tpu_custom_call" | custom-call | tf_op jit(solution)/shard_map/spill/pallas_call | solution.py:526

commit v4 on v3

--- a/solution.py
+++ b/solution.py
@@ -18,8 +18,8 @@
 def kernel(
     nrow, nphi, rows, cells, tiles, cycles,
     widths_far, hydro, face, diffusion_far, O, F,
-    H, S, R, SF, RF, FN, Q, M, PX, OM, MG, E, EX,
-    widths, diffusion, small_sem, load_sem, send_phi, recv_phi, send_edge, recv_edge,
+    H, S, R, SF, RF, FN, Q, M, PX, OM, MG, E,
+    widths, diffusion, small_sem, load_sem, send_phi, recv_phi, send_face, recv_face,
     send_mean, recv_mean, send_row, recv_row, pair_ack, far_ack, row_ack,
 ):
     nvar = hydro.shape[0]
@@ -144,6 +144,16 @@
             near_copy(k).start()
     for c in loads[nvar:]:
         c.wait()
+    face_left = pltpu.make_async_remote_copy(
+        src_ref=SF, dst_ref=RF, send_sem=send_face, recv_sem=recv_face,
+        device_id={"phi": left}, device_id_type=MESH)
+    for t in range(tiles):
+        SF[t] = F[nface - 1, layer(0, 0, t), :]
+
+    @pl.when(odd == 1)
+    def _():
+        face_left.start()
+
 
     def polar_cells(r, b):
         value = jnp.zeros((SUB, LANES), jnp.float32)
@@ -172,8 +182,6 @@
     mean_near.start()
     for k in range(EARLY, MIDDLE):
         near_copy(k).start()
-    for t in range(tiles):
-        SF[t] = F[nface - 1, layer(0, 0, t), :]
 
     for c in small:
         c.wait()
@@ -211,19 +219,18 @@
 
     lax.fori_loop(0, rows, local_average, 0, unroll=2)
 
-    def edge_copy(way, target):
-        return pltpu.make_async_remote_copy(
-            src_ref=E.at[way], dst_ref=EX.at[way], send_sem=send_edge.at[way], recv_sem=recv_edge.at[way],
-            device_id={"phi": target}, device_id_type=MESH)
-
-    face_left = pltpu.make_async_remote_copy(
-        src_ref=SF, dst_ref=RF, send_sem=send_edge.at[2], recv_sem=recv_edge.at[2],
-        device_id={"phi": left}, device_id_type=MESH)
-    edge_copy(near_way, partner).start()
-
-    @pl.when(odd == 1)
-    def _():
-        face_left.start()
+    def put_edges(way, k, i, f, source):
+        edges = unpack(E[source], f)
+        S[way, k, i, 0] = jnp.where(low, edges, S[way, k, i, 0])
+        S[way, k, i, last] = jnp.where(high, edges, S[way, k, i, last])
+
+    for k in range(MIDDLE, nvar):
+        for way in range(2):
+            put_edges(way, k, 0, k, way)
+    for k in range(MIDDLE):
+        put_edges(far_way, k, 0, k, far_way)
+        put_edges(near_way, k + MIDDLE, 1, k, near_way)
+    put_edges(0, nvar - 1, 1, fields - 1, 0)
 
     for k in range(MIDDLE, nvar):
         near_copy(k).start()
@@ -243,10 +250,11 @@
         def _():
             pl.semaphore_wait(far_ack, 1)
 
-        edge_copy(far_way, far).start()
-
         @pl.when(odd == 0)
         def _():
+            edges = unpack(E[0], fields - 1)
+            SF[0] = jnp.where(low, edges, SF[0])
+            SF[last] = jnp.where(high, edges, SF[last])
             face_left.start()
 
         for k in range(nvar):
@@ -295,7 +303,6 @@
 
     for r in (0, 1, rows - 2, rows - 1):
         spread(r)
-    lax.fori_loop(2, rows - 2, lambda r, c: (spread(r), c)[1], 0, unroll=4)
 
     down = pltpu.make_async_remote_copy(
         src_ref=H.at[:, pl.ds(2 * ring, 2 * ring)], dst_ref=H.at[:, pl.ds((rows + 2) * ring, 2 * ring)],
@@ -316,6 +323,8 @@
     def _():
         pl.semaphore_wait(row_ack, 1)
         up.start()
+
+    lax.fori_loop(2, rows - 2, lambda r, c: (spread(r), c)[1], 0, unroll=4)
 
     @pl.when(row == 0)
     def _():
@@ -389,11 +398,7 @@
     for r in (0, 1, rows - 2, rows - 1):
         smooth_row(r)
 
-    edge_copy(1, right).wait_recv()
-    edge_copy(0, left).wait_recv()
-    local = width <= cells
-    from_left = jnp.where(local, EX[1], next_hi)
-    from_right = jnp.where(local, EX[0], next_lo)
+    local = unpack(width, 0) <= cells
 
     def fixed(raw, edge, t):
         if t == 0:
@@ -402,18 +407,18 @@
             raw = jnp.where(high, edge, raw)
         return raw
 
-    face_left.wait_recv()
-    edge_f = unpack(from_right, fields - 1)
-    for t in range(tiles):
-        O[fields - 1, layer(0, cells - 1, t), :] = 0.5 * (F[nface - 1, layer(0, cells - 1, t), :] + fixed(RF[t], edge_f, t))
-
-    for k in range(nvar):
-        halo(1, right, k).wait_recv()
-        halo(0, left, k).wait_recv()
-        edge_l = unpack(from_left, k)
-        edge_r = unpack(from_right, k)
+    def sent_edge(way, k, t):
+        if k >= MIDDLE:
+            return R[way, k, 0, t]
+        return jnp.where(odd == way, R[way, k + MIDDLE, 1, t], R[way, k, 0, t])
+
+    def patch(k):
+        mean_l = unpack(next_hi, k)
+        mean_r = unpack(next_lo, k)
         for t in range(tiles):
             scale = diffusion[k : k + 1, part(t)] * (1.0 / 12.0)
+            edge_l = jnp.where(local, sent_edge(1, k, t), mean_l)
+            edge_r = jnp.where(local, sent_edge(0, k, t), mean_r)
             l1 = fixed(R[1, k, 1, t], edge_l, t) - H[k, layer(2, cells - 1, t), :]
             l2 = fixed(R[1, k, 0, t], edge_l, t) - H[k, layer(2, cells - 2, t), :]
             r1 = fixed(R[0, k, 0, t], edge_r, t) - H[k, layer(2, 0, t), :]
@@ -421,11 +426,26 @@
             for cell, term in ((0, 16.0 * l1 - l2), (1, -l1), (cells - 2, -r1), (cells - 1, 16.0 * r1 - r2)):
                 O[k, layer(0, cell, t), :] = O[k, layer(0, cell, t), :] + scale * term
 
+    def arrive(k):
+        halo(1, right, k).wait_recv()
+        halo(0, left, k).wait_recv()
+
+    for k in range(MIDDLE):
+        arrive(k)
+    face_left.wait_recv()
+    for k in range(MIDDLE, nvar):
+        arrive(k)
+        if k < 2 * MIDDLE:
+            patch(k - MIDDLE)
+        patch(k)
+    mean_f = unpack(next_lo, fields - 1)
+    for t in range(tiles):
+        edge_f = jnp.where(local, jnp.where(odd == 0, R[0, nvar - 1, 1, t], RF[t]), mean_f)
+        O[fields - 1, layer(0, cells - 1, t), :] = 0.5 * (F[nface - 1, layer(0, cells - 1, t), :] + fixed(RF[t], edge_f, t))
+
     for k in range(nvar):
         near_copy(k).wait_send()
         far_copy(k).wait_send()
-    edge_copy(near_way, partner).wait_send()
-    edge_copy(far_way, far).wait_send()
     face_left.wait_send()
     mean_near.wait_send()
     for step in range(1, pairs):
@@ -500,15 +520,14 @@
             shape(rows, LANES),
             shape(nphi // 2, rows, LANES),
             shape(2, rows, LANES),
-            shape(2, rows, LANES),
             pltpu.SMEM((2 * cycles,), jnp.int32),
             shape(nvar, theta),
             pltpu.SemaphoreType.DMA((2,)),
             pltpu.SemaphoreType.DMA((fields,)),
             pltpu.SemaphoreType.DMA((2, nvar)),
             pltpu.SemaphoreType.DMA((2, nvar)),
-            pltpu.SemaphoreType.DMA((3,)),
-            pltpu.SemaphoreType.DMA((3,)),
+            pltpu.SemaphoreType.DMA,
+            pltpu.SemaphoreType.DMA,
             pltpu.SemaphoreType.DMA((nphi // 2,)),
             pltpu.SemaphoreType.DMA((nphi // 2,)),
             pltpu.SemaphoreType.DMA((3,)),
@@ -522,7 +541,7 @@
         ),
         name="step",
     )(widths, blocked(hydro_vars), blocked(face_b), diffusion)
-    pieces = 2
+    pieces = 1
     conserved, faces = pl.pallas_call(
         functools.partial(spill, pieces),
         out_shape=(

time: 25.5 us -> 24.2 us (0.949)
  Pallas kernels: 24.7 us -> 23.4 us
    pallas_call x1, Pallas kernels: 22 us -> 20.8 us  [body(): pl.pallas_call(functools.partial(kernel, nrow, nphi, rows, cells, tiles,...]
where the time goes in v4:
time: 24.2 us; the launch traced here: 24.1 us
  Pallas kernels  23.4 us (97%)
  between operations  0.64 us (3%)
    pallas_call x1, Pallas kernels, body(): pl.pallas_call(functools.partial(kernel, nrow, nphi, rows, cells, tiles,...  20.8 us
    pallas_call x1, Pallas kernels, body(): pl.pallas_call(functools.partial(spill, pieces), out_shape=(jax.ShapeDtyp...  2.59 us

profile of v4, /device:TPU:0, one launch (start us, length us, event | category | flops | bytes accessed | tf_op | source)
XLA Modules:
  0.0 24.1 jit_solution(5991069116074815739)
XLA Ops:
  0.6 20.8 %step.1 = (f32[8,1024,128]{2,1,0:T(8,128)S(1)}, f32[3,1024,128]{2,1,0:T(8,128)S(1)}) custom-call(s32[16]{0:T(128)} %widths_far.1, f32[5,1024,128]{2,1,0:T(8,128)} %bitcast.20, f32[3,1024,128]{2,1,0:T(8,128)} %bitcast.21, f32[5,256]{1,0:T(8,128)} %diffusion_far.1), custom_call_target="tpu_custom_call" | custom-call | tf_op jit(solution)/shard_map/step/pallas_call | solution.py:502
  21.5 2.6 %spill.1 = (f32[8,1024,128]{2,1,0:T(8,128)}, f32[3,1024,128]{2,1,0:T(8,128)}) custom-call(f32[8,1024,128]{2,1,0:T(8,128)S(1)} %get-tuple-element.6.conserved, f32[3,1024,128]{2,1,0:T(8,128)S(1)} %get-tuple-element.7.faces), custom_call_target="tpu_custom_call" | custom-call | tf_op jit(solution)/shard_map/spill/pallas_call | solution.py:545

commit v5 on v4

--- a/solution.py
+++ b/solution.py
@@ -15,9 +15,36 @@
 LIMIT = 58000000
 
 
+def late_slots(tiles):
+    names = ["halo", "inner", "face", "face_edge", "scale"]
+    sizes = [4 * tiles, 4 * tiles, tiles, tiles, tiles]
+    starts, total = {}, 0
+    for name, size in zip(names, sizes):
+        starts[name] = total
+        total += size
+    for name in ("mean_left", "mean_right", "mean_face", "local"):
+        starts[name] = total
+        total += 1
+    return starts, total
+
+
+def fix_polar(low, high, last, raw, edge, t):
+    if t == 0:
+        raw = jnp.where(low, edge, raw)
+    if t == last:
+        raw = jnp.where(high, edge, raw)
+    return raw
+
+
+def halo_terms(scale, from_left, from_right, inner):
+    l1, l2 = from_left[1] - inner[3], from_left[0] - inner[2]
+    r1, r2 = from_right[0] - inner[0], from_right[1] - inner[1]
+    return [scale * term for term in (16.0 * l1 - l2, -l1, -r1, 16.0 * r1 - r2)]
+
+
 def kernel(
     nrow, nphi, rows, cells, tiles, cycles,
-    widths_far, hydro, face, diffusion_far, O, F,
+    widths_far, hydro, face, diffusion_far, O, F, A,
     H, S, R, SF, RF, FN, Q, M, PX, OM, MG, E,
     widths, diffusion, small_sem, load_sem, send_phi, recv_phi, send_face, recv_face,
     send_mean, recv_mean, send_row, recv_row, pair_ack, far_ack, row_ack,
@@ -142,6 +169,12 @@
 
         if k < EARLY:
             near_copy(k).start()
+        if k < MIDDLE:
+
+            @pl.when(phi == nphi - 1)
+            def _(k=k):
+                far_copy(k).start()
+
     for c in loads[nvar:]:
         c.wait()
     face_left = pltpu.make_async_remote_copy(
@@ -227,9 +260,8 @@
     for k in range(MIDDLE, nvar):
         for way in range(2):
             put_edges(way, k, 0, k, way)
-    for k in range(MIDDLE):
-        put_edges(far_way, k, 0, k, far_way)
-        put_edges(near_way, k + MIDDLE, 1, k, near_way)
+            if k < 2 * MIDDLE:
+                put_edges(way, k, 1, k - MIDDLE, way)
     put_edges(0, nvar - 1, 1, fields - 1, 0)
 
     for k in range(MIDDLE, nvar):
@@ -257,7 +289,12 @@
             SF[last] = jnp.where(high, edges, SF[last])
             face_left.start()
 
-        for k in range(nvar):
+        @pl.when(phi < nphi - 1)
+        def _():
+            for k in range(MIDDLE):
+                far_copy(k).start()
+
+        for k in range(MIDDLE, nvar):
             far_copy(k).start()
 
     @pl.when(phi > 0)
@@ -399,49 +436,55 @@
         smooth_row(r)
 
     local = unpack(width, 0) <= cells
-
-    def fixed(raw, edge, t):
-        if t == 0:
-            raw = jnp.where(low, edge, raw)
-        if t == last:
-            raw = jnp.where(high, edge, raw)
-        return raw
+    ends = (0, 1, cells - 2, cells - 1)
 
     def sent_edge(way, k, t):
-        if k >= MIDDLE:
-            return R[way, k, 0, t]
-        return jnp.where(odd == way, R[way, k + MIDDLE, 1, t], R[way, k, 0, t])
+        return R[way, k, 0, t] if k >= MIDDLE else R[way, k + MIDDLE, 1, t]
 
     def patch(k):
         mean_l = unpack(next_hi, k)
         mean_r = unpack(next_lo, k)
         for t in range(tiles):
-            scale = diffusion[k : k + 1, part(t)] * (1.0 / 12.0)
             edge_l = jnp.where(local, sent_edge(1, k, t), mean_l)
             edge_r = jnp.where(local, sent_edge(0, k, t), mean_r)
-            l1 = fixed(R[1, k, 1, t], edge_l, t) - H[k, layer(2, cells - 1, t), :]
-            l2 = fixed(R[1, k, 0, t], edge_l, t) - H[k, layer(2, cells - 2, t), :]
-            r1 = fixed(R[0, k, 0, t], edge_r, t) - H[k, layer(2, 0, t), :]
-            r2 = fixed(R[0, k, 1, t], edge_r, t) - H[k, layer(2, 1, t), :]
-            for cell, term in ((0, 16.0 * l1 - l2), (1, -l1), (cells - 2, -r1), (cells - 1, 16.0 * r1 - r2)):
-                O[k, layer(0, cell, t), :] = O[k, layer(0, cell, t), :] + scale * term
+            terms = halo_terms(
+                diffusion[k : k + 1, part(t)] * (1.0 / 12.0),
+                [fix_polar(low, high, last, R[1, k, i, t], edge_l, t) for i in range(2)],
+                [fix_polar(low, high, last, R[0, k, i, t], edge_r, t) for i in range(2)],
+                [H[k, layer(2, cell, t), :] for cell in ends])
+            for cell, term in zip(ends, terms):
+                O[k, layer(0, cell, t), :] = O[k, layer(0, cell, t), :] + term
 
     def arrive(k):
         halo(1, right, k).wait_recv()
         halo(0, left, k).wait_recv()
 
+    slots, _ = late_slots(tiles)
+    final = nvar - 1
+    A[slots["mean_left"]] = unpack(next_hi, final)
+    A[slots["mean_right"]] = unpack(next_lo, final)
+    A[slots["mean_face"]] = unpack(next_lo, fields - 1)
+    A[slots["local"]] = jnp.broadcast_to(jnp.where(local, 1.0, 0.0), (rows, LANES))
+    for t in range(tiles):
+        A[slots["scale"] + t] = jnp.broadcast_to(diffusion[final : final + 1, part(t)] * (1.0 / 12.0), (rows, LANES))
+        for i, cell in enumerate(ends):
+            A[slots["inner"] + 4 * t + i] = H[final, layer(2, cell, t), :]
     for k in range(MIDDLE):
         arrive(k)
     face_left.wait_recv()
-    for k in range(MIDDLE, nvar):
+    for t in range(tiles):
+        A[slots["face"] + t] = RF[t]
+    for k in range(MIDDLE, final):
         arrive(k)
         if k < 2 * MIDDLE:
             patch(k - MIDDLE)
         patch(k)
-    mean_f = unpack(next_lo, fields - 1)
+    arrive(final)
     for t in range(tiles):
-        edge_f = jnp.where(local, jnp.where(odd == 0, R[0, nvar - 1, 1, t], RF[t]), mean_f)
-        O[fields - 1, layer(0, cells - 1, t), :] = 0.5 * (F[nface - 1, layer(0, cells - 1, t), :] + fixed(RF[t], edge_f, t))
+        A[slots["face_edge"] + t] = jnp.where(odd == 0, R[0, final, 1, t], RF[t])
+        for way in range(2):
+            for i in range(2):
+                A[slots["halo"] + 4 * t + 2 * way + i] = R[way, final, i, t]
 
     for k in range(nvar):
         near_copy(k).wait_send()
@@ -461,17 +504,51 @@
         up.wait_send()
 
 
-def spill(pieces, conserved, faces, conserved_out, faces_out, sem):
+def spill(nvar, rows, cells, tiles, cycles, conserved, faces, A, conserved_out, faces_out, P, sem):
     fields = conserved.shape[0]
-    size = conserved.shape[1] // pieces
-    copies = []
-    for k in range(fields + faces.shape[0]):
-        source, target, i = (conserved, conserved_out, k) if k < fields else (faces, faces_out, k - fields)
-        for p in range(pieces):
-            where = pl.ds(p * size, size)
-            copies.append(pltpu.make_async_copy(source.at[i, where], target.at[i, where], sem.at[k, p]))
+    nface = faces.shape[0]
+    ring = cells * tiles
+    last = tiles - 1
+    late = (nvar - 1, fields - 1)
+
+    def layer(cell, t):
+        return pl.ds((cell // SUB * tiles + t) * SUB + cell % SUB, rows, stride=ring)
+
+    def out(k, source):
+        return pltpu.make_async_copy(source, conserved_out.at[k], sem.at[k])
+
+    copies = [out(k, conserved.at[k]) for k in range(fields) if k not in late]
+    copies += [pltpu.make_async_copy(faces.at[k], faces_out.at[k], sem.at[fields + k]) for k in range(nface)]
     for c in copies:
         c.start()
+
+    slots, _ = late_slots(tiles)
+    lane = lax.broadcasted_iota(jnp.int32, (1, LANES), 1)
+    low = lane < cycles
+    high = lane >= LANES - cycles
+    local = A[slots["local"]] > 0.5
+    ends = (0, 1, cells - 2, cells - 1)
+    for n, k in enumerate(late):
+        P[n] = conserved[k]
+    for t in range(tiles):
+        halo = [A[slots["halo"] + 4 * t + i] for i in range(4)]
+        edge_l = jnp.where(local, halo[2], A[slots["mean_left"]])
+        edge_r = jnp.where(local, halo[0], A[slots["mean_right"]])
+        terms = halo_terms(
+            A[slots["scale"] + t],
+            [fix_polar(low, high, last, v, edge_l, t) for v in halo[2:]],
+            [fix_polar(low, high, last, v, edge_r, t) for v in halo[:2]],
+            [A[slots["inner"] + 4 * t + i] for i in range(4)])
+        for cell, term in zip(ends, terms):
+            P[0, layer(cell, t), :] = P[0, layer(cell, t), :] + term
+    copies.append(out(late[0], P.at[0]))
+    copies[-1].start()
+    for t in range(tiles):
+        edge = jnp.where(local, A[slots["face_edge"] + t], A[slots["mean_face"]])
+        following = fix_polar(low, high, last, A[slots["face"] + t], edge, t)
+        P[1, layer(cells - 1, t), :] = 0.5 * (faces[nface - 1, layer(cells - 1, t), :] + following)
+    copies.append(out(late[1], P.at[1]))
+    copies[-1].start()
     for c in copies:
         c.wait()
 
@@ -498,15 +575,17 @@
     shape = lambda *s: pltpu.VMEM(s, f32)
     far = pl.BlockSpec(memory_space=pltpu.HBM)
     near = pl.BlockSpec(memory_space=pltpu.VMEM)
-    result_bytes = (fields + nface) * rows * ring * LANES * 4
-    conserved, faces = pl.pallas_call(
+    result_bytes = ((fields + nface) * ring + late_slots(tiles)[1]) * rows * LANES * 4
+    slots = late_slots(tiles)[1]
+    conserved, faces, late = pl.pallas_call(
         functools.partial(kernel, nrow, nphi, rows, cells, tiles, cycles),
         out_shape=(
             pltpu.VMEM((fields, rows * ring, LANES), f32),
             pltpu.VMEM((nface, rows * ring, LANES), f32),
+            pltpu.VMEM((slots, rows, LANES), f32),
         ),
         in_specs=[far, far, far, far],
-        out_specs=(near, near),
+        out_specs=(near, near, near),
         scratch_shapes=[
             shape(nvar, (rows + 4) * ring, LANES),
             shape(2, nvar, 2, tiles, rows, LANES),
@@ -541,19 +620,18 @@
         ),
         name="step",
     )(widths, blocked(hydro_vars), blocked(face_b), diffusion)
-    pieces = 1
     conserved, faces = pl.pallas_call(
-        functools.partial(spill, pieces),
+        functools.partial(spill, nvar, rows, cells, tiles, cycles),
         out_shape=(
             jax.ShapeDtypeStruct((fields, rows * ring, LANES), f32),
             jax.ShapeDtypeStruct((nface, rows * ring, LANES), f32),
         ),
-        in_specs=[near, near],
+        in_specs=[near, near, near],
         out_specs=(far, far),
-        scratch_shapes=[pltpu.SemaphoreType.DMA((fields + nface, pieces))],
-        compiler_params=pltpu.CompilerParams(vmem_limit_bytes=1000000),
+        scratch_shapes=[shape(2, rows * ring, LANES), pltpu.SemaphoreType.DMA((fields + nface,))],
+        compiler_params=pltpu.CompilerParams(vmem_limit_bytes=8 * rows * ring * LANES + 2000000),
         name="spill",
-    )(conserved, faces)
+    )(conserved, faces, late)
     return unblocked(conserved, rows, cells, theta), unblocked(faces, rows, cells, theta)
 
 

time: 24.2 us -> 23.9 us (0.988)
  Pallas kernels: 23.4 us -> 23.1 us
    pallas_call x1, Pallas kernels: 20.8 us -> 20.6 us  [body(): pl.pallas_call(functools.partial(kernel, nrow, nphi, rows, cells, tiles,...]
where the time goes in v5:
time: 23.9 us; the launch traced here: 23.8 us
  Pallas kernels  23.1 us (97%)
  between operations  0.64 us (3%)
    pallas_call x1, Pallas kernels, body(): pl.pallas_call(functools.partial(kernel, nrow, nphi, rows, cells, tiles,...  20.6 us
    pallas_call x1, Pallas kernels, body(): pl.pallas_call(functools.partial(spill, nvar, rows, cells, tiles, cycles)...  2.59 us

profile of v5, /device:TPU:0, one launch (start us, length us, event | category | flops | bytes accessed | tf_op | source)
XLA Modules:
  0.0 23.8 jit_solution(11249456290285547368)
XLA Ops:
  0.6 20.6 %step.1 = (f32[8,1024,128]{2,1,0:T(8,128)S(1)}, f32[3,1024,128]{2,1,0:T(8,128)S(1)}, f32[26,32,128]{2,1,0:T(8,128)S(1)}) custom-call(s32[16]{0:T(128)} %widths_far.1, f32[5,1024,128]{2,1,0:T(8,128)} %bitcast.20, f32[3,1024,128]{2,1,0:T(8,128)} %bitcast.21, f32[5,256]{1,0:T(8,128)} %diffusion_far.1), custom_call_target="tpu_custom_call" | custom-call | tf_op jit(solution)/shard_map/step/pallas_call | solution.py:580
  21.2 2.6 %spill.1 = (f32[8,1024,128]{2,1,0:T(8,128)}, f32[3,1024,128]{2,1,0:T(8,128)}) custom-call(f32[8,1024,128]{2,1,0:T(8,128)S(1)} %get-tuple-element.7.conserved, f32[3,1024,128]{2,1,0:T(8,128)S(1)} %get-tuple-element.8.faces, f32[26,32,128]{2,1,0:T(8,128)S(1)} %get-tuple-element.9.A), custom_call_target="tpu_custom_call" | custom-call | tf_op jit(solution)/shard_map/spill/pallas_call | solution.py:623

commit v6 on v5

--- a/solution.py
+++ b/solution.py
@@ -12,6 +12,8 @@
 SUB = 8
 EARLY = 1
 MIDDLE = 2
+HELD_NEAR = 2
+HELD_FAR = 2
 LIMIT = 58000000
 
 
@@ -65,6 +67,8 @@
     partner = phi + 1 - 2 * odd
     far = jnp.where(odd == 1, right, left)
     near_way, far_way = 1 - odd, odd
+    yields_near = (phi == 1) & (lax.rem(row, 2) == 1)
+    yields_far = (phi == nphi - 1) & (lax.rem(row, 2) == 1)
     packed = 2 * cycles
 
     loads = [pltpu.make_async_copy(hydro.at[k], H.at[k, pl.ds(2 * ring, rows * ring)], load_sem.at[k]) for k in range(nvar)]
@@ -264,8 +268,14 @@
                 put_edges(way, k, 1, k - MIDDLE, way)
     put_edges(0, nvar - 1, 1, fields - 1, 0)
 
-    for k in range(MIDDLE, nvar):
+    for k in range(MIDDLE, HELD_NEAR):
         near_copy(k).start()
+
+    @pl.when(jnp.logical_not(yields_near))
+    def _():
+        for k in range(HELD_NEAR, nvar):
+            near_copy(k).start()
+
 
     mean_near.wait_recv()
     MG[pair] = (M[...] + PX[...]) * 0.5
@@ -294,8 +304,13 @@
             for k in range(MIDDLE):
                 far_copy(k).start()
 
-        for k in range(MIDDLE, nvar):
+        for k in range(MIDDLE, HELD_FAR):
             far_copy(k).start()
+
+        @pl.when(jnp.logical_not(yields_far))
+        def _():
+            for k in range(HELD_FAR, nvar):
+                far_copy(k).start()
 
     @pl.when(phi > 0)
     def _():
@@ -362,6 +377,16 @@
         up.start()
 
     lax.fori_loop(2, rows - 2, lambda r, c: (spread(r), c)[1], 0, unroll=4)
+
+    @pl.when(yields_near)
+    def _():
+        for k in range(HELD_NEAR, nvar):
+            near_copy(k).start()
+
+    @pl.when(yields_far)
+    def _():
+        for k in range(HELD_FAR, nvar):
+            far_copy(k).start()
 
     @pl.when(row == 0)
     def _():
@@ -418,7 +443,7 @@
         smooth_row(r)
         return carry
 
-    lax.fori_loop(2, rows - 2, inner_row, 0, unroll=2)
+    lax.fori_loop(2, rows - 2, inner_row, 0, unroll=4)
     for r in (0, 1, rows - 2):
         field_row(r, lambda t, r=r: whole(F, 0, r + 1, t))
 

time: 23.9 us -> 23.3 us (0.975)
  Pallas kernels: 23.1 us -> 22.4 us
    pallas_call x1, Pallas kernels: 20.6 us -> 19.8 us  [body(): pl.pallas_call(functools.partial(kernel, nrow, nphi, rows, cells, tiles,...]
where the time goes in v6:
time: 23.3 us; the launch traced here: 23 us
  Pallas kernels  22.4 us (96%)
  between operations  0.64 us (3%)
    pallas_call x1, Pallas kernels, body(): pl.pallas_call(functools.partial(kernel, nrow, nphi, rows, cells, tiles,...  19.8 us
    pallas_call x1, Pallas kernels, body(): pl.pallas_call(functools.partial(spill, nvar, rows, cells, tiles, cycles)...  2.59 us

profile of v6, /device:TPU:0, one launch (start us, length us, event | category | flops | bytes accessed | tf_op | source)
XLA Modules:
  0.0 23.0 jit_solution(11162563546990243460)
XLA Ops:
  0.6 19.8 %step.1 = (f32[8,1024,128]{2,1,0:T(8,128)S(1)}, f32[3,1024,128]{2,1,0:T(8,128)S(1)}, f32[26,32,128]{2,1,0:T(8,128)S(1)}) custom-call(s32[16]{0:T(128)} %widths_far.1, f32[5,1024,128]{2,1,0:T(8,128)} %bitcast.20, f32[3,1024,128]{2,1,0:T(8,128)} %bitcast.21, f32[5,256]{1,0:T(8,128)} %diffusion_far.1), custom_call_target="tpu_custom_call" | custom-call | tf_op jit(solution)/shard_map/step/pallas_call | solution.py:605
  20.5 2.6 %spill.1 = (f32[8,1024,128]{2,1,0:T(8,128)}, f32[3,1024,128]{2,1,0:T(8,128)}) custom-call(f32[8,1024,128]{2,1,0:T(8,128)S(1)} %get-tuple-element.7.conserved, f32[3,1024,128]{2,1,0:T(8,128)S(1)} %get-tuple-element.8.faces, f32[26,32,128]{2,1,0:T(8,128)S(1)} %get-tuple-element.9.A), custom_call_target="tpu_custom_call" | custom-call | tf_op jit(solution)/shard_map/spill/pallas_call | solution.py:648

commit v7 on v6

--- a/solution.py
+++ b/solution.py
@@ -14,20 +14,22 @@
 MIDDLE = 2
 HELD_NEAR = 2
 HELD_FAR = 2
+LATE = (0, 1, 2, 3, 4)
 LIMIT = 58000000
 
 
-def late_slots(tiles):
-    names = ["halo", "inner", "face", "face_edge", "scale"]
-    sizes = [4 * tiles, 4 * tiles, tiles, tiles, tiles]
+def late_slots(nvar, tiles):
+    names = ("mean_left", "mean_right", "scale", "mean_face", "local", "odd")
+    sizes = (nvar, nvar, nvar * tiles, 1, 1, 1)
     starts, total = {}, 0
     for name, size in zip(names, sizes):
         starts[name] = total
         total += size
-    for name in ("mean_left", "mean_right", "mean_face", "local"):
-        starts[name] = total
-        total += 1
     return starts, total
+
+
+def sent_edge(R, way, k, t):
+    return R[way, k, 0, t] if k >= MIDDLE else R[way, k + MIDDLE, 1, t]
 
 
 def fix_polar(low, high, last, raw, edge, t):
@@ -46,8 +48,8 @@
 
 def kernel(
     nrow, nphi, rows, cells, tiles, cycles,
-    widths_far, hydro, face, diffusion_far, O, F, A,
-    H, S, R, SF, RF, FN, Q, M, PX, OM, MG, E,
+    widths_far, hydro, face, diffusion_far, O, F, A, H, R, RF,
+    S, SF, FN, Q, M, PX, OM, MG, E,
     widths, diffusion, small_sem, load_sem, send_phi, recv_phi, send_face, recv_face,
     send_mean, recv_mean, send_row, recv_row, pair_ack, far_ack, row_ack,
 ):
@@ -463,15 +465,12 @@
     local = unpack(width, 0) <= cells
     ends = (0, 1, cells - 2, cells - 1)
 
-    def sent_edge(way, k, t):
-        return R[way, k, 0, t] if k >= MIDDLE else R[way, k + MIDDLE, 1, t]
-
     def patch(k):
         mean_l = unpack(next_hi, k)
         mean_r = unpack(next_lo, k)
         for t in range(tiles):
-            edge_l = jnp.where(local, sent_edge(1, k, t), mean_l)
-            edge_r = jnp.where(local, sent_edge(0, k, t), mean_r)
+            edge_l = jnp.where(local, sent_edge(R, 1, k, t), mean_l)
+            edge_r = jnp.where(local, sent_edge(R, 0, k, t), mean_r)
             terms = halo_terms(
                 diffusion[k : k + 1, part(t)] * (1.0 / 12.0),
                 [fix_polar(low, high, last, R[1, k, i, t], edge_l, t) for i in range(2)],
@@ -484,32 +483,25 @@
         halo(1, right, k).wait_recv()
         halo(0, left, k).wait_recv()
 
-    slots, _ = late_slots(tiles)
-    final = nvar - 1
-    A[slots["mean_left"]] = unpack(next_hi, final)
-    A[slots["mean_right"]] = unpack(next_lo, final)
+    slots, _ = late_slots(nvar, tiles)
+    for k in range(nvar):
+        if k in LATE:
+            A[slots["mean_left"] + k] = unpack(next_hi, k)
+            A[slots["mean_right"] + k] = unpack(next_lo, k)
+            for t in range(tiles):
+                A[slots["scale"] + k * tiles + t] = jnp.broadcast_to(
+                    diffusion[k : k + 1, part(t)] * (1.0 / 12.0), (rows, LANES))
     A[slots["mean_face"]] = unpack(next_lo, fields - 1)
     A[slots["local"]] = jnp.broadcast_to(jnp.where(local, 1.0, 0.0), (rows, LANES))
-    for t in range(tiles):
-        A[slots["scale"] + t] = jnp.broadcast_to(diffusion[final : final + 1, part(t)] * (1.0 / 12.0), (rows, LANES))
-        for i, cell in enumerate(ends):
-            A[slots["inner"] + 4 * t + i] = H[final, layer(2, cell, t), :]
+    A[slots["odd"]] = jnp.full((rows, LANES), odd, jnp.int32).astype(jnp.float32)
     for k in range(MIDDLE):
         arrive(k)
     face_left.wait_recv()
-    for t in range(tiles):
-        A[slots["face"] + t] = RF[t]
-    for k in range(MIDDLE, final):
+    for k in range(MIDDLE, nvar):
         arrive(k)
-        if k < 2 * MIDDLE:
-            patch(k - MIDDLE)
-        patch(k)
-    arrive(final)
-    for t in range(tiles):
-        A[slots["face_edge"] + t] = jnp.where(odd == 0, R[0, final, 1, t], RF[t])
-        for way in range(2):
-            for i in range(2):
-                A[slots["halo"] + 4 * t + 2 * way + i] = R[way, final, i, t]
+        for n in (k - MIDDLE, k):
+            if n not in LATE and (n < MIDDLE or n == k):
+                patch(n)
 
     for k in range(nvar):
         near_copy(k).wait_send()
@@ -529,51 +521,54 @@
         up.wait_send()
 
 
-def spill(nvar, rows, cells, tiles, cycles, conserved, faces, A, conserved_out, faces_out, P, sem):
+def spill(nvar, rows, cells, tiles, cycles, conserved, faces, A, H, R, RF, conserved_out, faces_out, P, sem):
     fields = conserved.shape[0]
     nface = faces.shape[0]
     ring = cells * tiles
     last = tiles - 1
-    late = (nvar - 1, fields - 1)
-
-    def layer(cell, t):
-        return pl.ds((cell // SUB * tiles + t) * SUB + cell % SUB, rows, stride=ring)
+    late = LATE + (fields - 1,)
+
+    def layer(r, cell, t):
+        return pl.ds(r * ring + (cell // SUB * tiles + t) * SUB + cell % SUB, rows, stride=ring)
 
     def out(k, source):
         return pltpu.make_async_copy(source, conserved_out.at[k], sem.at[k])
 
-    copies = [out(k, conserved.at[k]) for k in range(fields) if k not in late]
-    copies += [pltpu.make_async_copy(faces.at[k], faces_out.at[k], sem.at[fields + k]) for k in range(nface)]
+    copies = [pltpu.make_async_copy(faces.at[k], faces_out.at[k], sem.at[fields + k]) for k in range(nface)]
+    copies += [out(k, conserved.at[k]) for k in range(fields) if k not in late]
     for c in copies:
         c.start()
 
-    slots, _ = late_slots(tiles)
+    slots, _ = late_slots(nvar, tiles)
     lane = lax.broadcasted_iota(jnp.int32, (1, LANES), 1)
     low = lane < cycles
     high = lane >= LANES - cycles
     local = A[slots["local"]] > 0.5
+    odd = A[slots["odd"]] > 0.5
     ends = (0, 1, cells - 2, cells - 1)
-    for n, k in enumerate(late):
+    slot = len(LATE)
+    P[slot] = conserved[fields - 1]
+    for t in range(tiles):
+        edge = jnp.where(odd, RF[t], R[0, nvar - 1, 1, t])
+        edge = jnp.where(local, edge, A[slots["mean_face"]])
+        following = fix_polar(low, high, last, RF[t], edge, t)
+        P[slot, layer(0, cells - 1, t), :] = 0.5 * (faces[nface - 1, layer(0, cells - 1, t), :] + following)
+    copies.append(out(fields - 1, P.at[slot]))
+    copies[-1].start()
+    for n, k in enumerate(LATE):
         P[n] = conserved[k]
-    for t in range(tiles):
-        halo = [A[slots["halo"] + 4 * t + i] for i in range(4)]
-        edge_l = jnp.where(local, halo[2], A[slots["mean_left"]])
-        edge_r = jnp.where(local, halo[0], A[slots["mean_right"]])
-        terms = halo_terms(
-            A[slots["scale"] + t],
-            [fix_polar(low, high, last, v, edge_l, t) for v in halo[2:]],
-            [fix_polar(low, high, last, v, edge_r, t) for v in halo[:2]],
-            [A[slots["inner"] + 4 * t + i] for i in range(4)])
-        for cell, term in zip(ends, terms):
-            P[0, layer(cell, t), :] = P[0, layer(cell, t), :] + term
-    copies.append(out(late[0], P.at[0]))
-    copies[-1].start()
-    for t in range(tiles):
-        edge = jnp.where(local, A[slots["face_edge"] + t], A[slots["mean_face"]])
-        following = fix_polar(low, high, last, A[slots["face"] + t], edge, t)
-        P[1, layer(cells - 1, t), :] = 0.5 * (faces[nface - 1, layer(cells - 1, t), :] + following)
-    copies.append(out(late[1], P.at[1]))
-    copies[-1].start()
+        for t in range(tiles):
+            edge_l = jnp.where(local, sent_edge(R, 1, k, t), A[slots["mean_left"] + k])
+            edge_r = jnp.where(local, sent_edge(R, 0, k, t), A[slots["mean_right"] + k])
+            terms = halo_terms(
+                A[slots["scale"] + k * tiles + t],
+                [fix_polar(low, high, last, R[1, k, i, t], edge_l, t) for i in range(2)],
+                [fix_polar(low, high, last, R[0, k, i, t], edge_r, t) for i in range(2)],
+                [H[k, layer(2, cell, t), :] for cell in ends])
+            for cell, term in zip(ends, terms):
+                P[n, layer(0, cell, t), :] = P[n, layer(0, cell, t), :] + term
+        copies.append(out(k, P.at[n]))
+        copies[-1].start()
     for c in copies:
         c.wait()
 
@@ -600,22 +595,23 @@
     shape = lambda *s: pltpu.VMEM(s, f32)
     far = pl.BlockSpec(memory_space=pltpu.HBM)
     near = pl.BlockSpec(memory_space=pltpu.VMEM)
-    result_bytes = ((fields + nface) * ring + late_slots(tiles)[1]) * rows * LANES * 4
-    slots = late_slots(tiles)[1]
-    conserved, faces, late = pl.pallas_call(
+    slots = late_slots(nvar, tiles)[1]
+    held = ((fields + nface) * rows + nvar * (rows + 4)) * ring + (slots + (4 * nvar + 1) * tiles) * rows
+    result_bytes = held * LANES * 4
+    conserved, faces, *late = pl.pallas_call(
         functools.partial(kernel, nrow, nphi, rows, cells, tiles, cycles),
         out_shape=(
             pltpu.VMEM((fields, rows * ring, LANES), f32),
             pltpu.VMEM((nface, rows * ring, LANES), f32),
             pltpu.VMEM((slots, rows, LANES), f32),
+            shape(nvar, (rows + 4) * ring, LANES),
+            shape(2, nvar, 2, tiles, rows, LANES),
+            shape(tiles, rows, LANES),
         ),
         in_specs=[far, far, far, far],
-        out_specs=(near, near, near),
+        out_specs=(near,) * 6,
         scratch_shapes=[
-            shape(nvar, (rows + 4) * ring, LANES),
             shape(2, nvar, 2, tiles, rows, LANES),
-            shape(2, nvar, 2, tiles, rows, LANES),
-            shape(tiles, rows, LANES),
             shape(tiles, rows, LANES),
             shape(ring, LANES),
             shape(rows * cells, LANES),
@@ -651,12 +647,12 @@
             jax.ShapeDtypeStruct((fields, rows * ring, LANES), f32),
             jax.ShapeDtypeStruct((nface, rows * ring, LANES), f32),
         ),
-        in_specs=[near, near, near],
+        in_specs=[near] * 6,
         out_specs=(far, far),
-        scratch_shapes=[shape(2, rows * ring, LANES), pltpu.SemaphoreType.DMA((fields + nface,))],
-        compiler_params=pltpu.CompilerParams(vmem_limit_bytes=8 * rows * ring * LANES + 2000000),
+        scratch_shapes=[shape(len(LATE) + 1, rows * ring, LANES), pltpu.SemaphoreType.DMA((fields + nface,))],
+        compiler_params=pltpu.CompilerParams(vmem_limit_bytes=4 * (len(LATE) + 1) * rows * ring * LANES + 2000000),
         name="spill",
-    )(conserved, faces, late)
+    )(conserved, faces, *late)
     return unblocked(conserved, rows, cells, theta), unblocked(faces, rows, cells, theta)
 
 

time: 23.3 us -> 23.3 us (level)
  the two profiles are of different devices: /device:TPU:0 before, /device:TPU:1 now
where the time goes in v7:
time: 23.3 us; the launch traced here: 23.1 us
  Pallas kernels  22.5 us (97%)
  between operations  0.64 us (3%)
    pallas_call x1, Pallas kernels, body(): pl.pallas_call(functools.partial(kernel, nrow, nphi, rows, cells, tiles,...  19.9 us
    pallas_call x1, Pallas kernels, body(): pl.pallas_call(functools.partial(spill, nvar, rows, cells, tiles, cycles)...  2.59 us

profile of v7, /device:TPU:1, one launch (start us, length us, event | category | flops | bytes accessed | tf_op | source)
XLA Modules:
  0.0 23.1 jit_solution(2393805803736688176)
XLA Ops:
  0.6 19.9 %step.1 = (f32[8,1024,128]{2,1,0:T(8,128)S(1)}, f32[3,1024,128]{2,1,0:T(8,128)S(1)}, f32[23,32,128]{2,1,0:T(8,128)S(1)}, f32[5,1152,128]{2,1,0:T(8,128)S(1)}, f3...) custom-call(s32[16]{0:T(128)} %widths_far.1, f32[5,1024,128]{2,1,0:T(8,128)} %bitcast.20, ...), custom_call_target="tpu_custom_call" | custom-call | tf_op jit(solution)/shard_map/step/pallas_call | solution.py:601
  20.5 2.6 %spill.1 = (f32[8,1024,128]{2,1,0:T(8,128)}, f32[3,1024,128]{2,1,0:T(8,128)}) custom-call(f32[8,1024,128]{2,1,0:T(8,128)S(1)} %get-tuple-element.10.conserved, f32[3,1024,128]{2,1,0:T(8,128)S(1)} %get-tuple-element.11.faces, f32[23,32,128]{2,1,0:T(8,128)S(1)} %get-tuple-element.12.A, f32[5,1152,128]{2,1,0:T(8,128)S(1)} %get-tuple-element.13.H, ...), custom_call_target="tpu_custom_call" | custom-call | tf_op jit(solution)/shard_map/spill/pallas_call | solution.py:644

commit v8 on v7

--- a/solution.py
+++ b/solution.py
@@ -14,7 +14,6 @@
 MIDDLE = 2
 HELD_NEAR = 2
 HELD_FAR = 2
-LATE = (0, 1, 2, 3, 4)
 LIMIT = 58000000
 
 
@@ -29,7 +28,8 @@
 
 
 def sent_edge(R, way, k, t):
-    return R[way, k, 0, t] if k >= MIDDLE else R[way, k + MIDDLE, 1, t]
+    early = k < MIDDLE
+    return R[way, jnp.where(early, k + MIDDLE, k), jnp.where(early, 1, 0), t]
 
 
 def fix_polar(low, high, last, raw, edge, t):
@@ -217,7 +217,7 @@
         M[pl.ds(r, 1), :] = value[0:1] * (1.0 / cells)
         return carry
 
-    lax.fori_loop(0, rows, cell_mean, 0, unroll=4)
+    lax.fori_loop(0, rows, cell_mean, 0, unroll=8)
     mean_near.start()
     for k in range(EARLY, MIDDLE):
         near_copy(k).start()
@@ -256,7 +256,7 @@
         E[1, pl.ds(r, 1), :] = results[blocks - 1][SUB - 1 : SUB]
         return carry
 
-    lax.fori_loop(0, rows, local_average, 0, unroll=2)
+    lax.fori_loop(0, rows, local_average, 0, unroll=4)
 
     def put_edges(way, k, i, f, source):
         edges = unpack(E[source], f)
@@ -318,14 +318,14 @@
     def _():
         start_far()
 
-    for step in range(pairs - 1, 1, -1):
+    for step in range(pairs - 1, 0, -1):
         mean_copy(step).wait_recv()
-
-    @pl.when(phi == 0)
-    def _():
-        start_far()
-
-    mean_copy(1).wait_recv()
+        if step == pairs - 1:
+
+            @pl.when(phi == 0)
+            def _():
+                start_far()
+
 
     def group_mean(who):
         result = MG[who // 2]
@@ -463,21 +463,6 @@
         smooth_row(r)
 
     local = unpack(width, 0) <= cells
-    ends = (0, 1, cells - 2, cells - 1)
-
-    def patch(k):
-        mean_l = unpack(next_hi, k)
-        mean_r = unpack(next_lo, k)
-        for t in range(tiles):
-            edge_l = jnp.where(local, sent_edge(R, 1, k, t), mean_l)
-            edge_r = jnp.where(local, sent_edge(R, 0, k, t), mean_r)
-            terms = halo_terms(
-                diffusion[k : k + 1, part(t)] * (1.0 / 12.0),
-                [fix_polar(low, high, last, R[1, k, i, t], edge_l, t) for i in range(2)],
-                [fix_polar(low, high, last, R[0, k, i, t], edge_r, t) for i in range(2)],
-                [H[k, layer(2, cell, t), :] for cell in ends])
-            for cell, term in zip(ends, terms):
-                O[k, layer(0, cell, t), :] = O[k, layer(0, cell, t), :] + term
 
     def arrive(k):
         halo(1, right, k).wait_recv()
@@ -485,26 +470,22 @@
 
     slots, _ = late_slots(nvar, tiles)
     for k in range(nvar):
-        if k in LATE:
-            A[slots["mean_left"] + k] = unpack(next_hi, k)
-            A[slots["mean_right"] + k] = unpack(next_lo, k)
-            for t in range(tiles):
-                A[slots["scale"] + k * tiles + t] = jnp.broadcast_to(
-                    diffusion[k : k + 1, part(t)] * (1.0 / 12.0), (rows, LANES))
+        A[slots["mean_left"] + k] = unpack(next_hi, k)
+        A[slots["mean_right"] + k] = unpack(next_lo, k)
+        for t in range(tiles):
+            A[slots["scale"] + k * tiles + t] = jnp.broadcast_to(
+                diffusion[k : k + 1, part(t)] * (1.0 / 12.0), (rows, LANES))
     A[slots["mean_face"]] = unpack(next_lo, fields - 1)
     A[slots["local"]] = jnp.broadcast_to(jnp.where(local, 1.0, 0.0), (rows, LANES))
     A[slots["odd"]] = jnp.full((rows, LANES), odd, jnp.int32).astype(jnp.float32)
     for k in range(MIDDLE):
         arrive(k)
     face_left.wait_recv()
-    for k in range(MIDDLE, nvar):
+    for k in range(MIDDLE, nvar - 1):
         arrive(k)
-        for n in (k - MIDDLE, k):
-            if n not in LATE and (n < MIDDLE or n == k):
-                patch(n)
-
     for k in range(nvar):
-        near_copy(k).wait_send()
+        if k < nvar - 1:
+            near_copy(k).wait_send()
         far_copy(k).wait_send()
     face_left.wait_send()
     mean_near.wait_send()
@@ -519,6 +500,8 @@
     @pl.when(row < nrow - 1)
     def _():
         up.wait_send()
+    arrive(nvar - 1)
+    near_copy(nvar - 1).wait_send()
 
 
 def spill(nvar, rows, cells, tiles, cycles, conserved, faces, A, H, R, RF, conserved_out, faces_out, P, sem):
@@ -526,7 +509,7 @@
     nface = faces.shape[0]
     ring = cells * tiles
     last = tiles - 1
-    late = LATE + (fields - 1,)
+    late = tuple(range(nvar)) + (fields - 1,)
 
     def layer(r, cell, t):
         return pl.ds(r * ring + (cell // SUB * tiles + t) * SUB + cell % SUB, rows, stride=ring)
@@ -546,8 +529,17 @@
     local = A[slots["local"]] > 0.5
     odd = A[slots["odd"]] > 0.5
     ends = (0, 1, cells - 2, cells - 1)
-    slot = len(LATE)
-    P[slot] = conserved[fields - 1]
+    slot = nvar
+
+    def copy_in(n, k):
+        def move(i, carry):
+            where = pl.ds(pl.multiple_of(i * 8 * SUB, 8 * SUB), 8 * SUB)
+            P[n, where, :] = conserved[k, where, :]
+            return carry
+
+        lax.fori_loop(0, rows * ring // (8 * SUB), move, 0, unroll=2)
+
+    copy_in(slot, fields - 1)
     for t in range(tiles):
         edge = jnp.where(odd, RF[t], R[0, nvar - 1, 1, t])
         edge = jnp.where(local, edge, A[slots["mean_face"]])
@@ -555,8 +547,8 @@
         P[slot, layer(0, cells - 1, t), :] = 0.5 * (faces[nface - 1, layer(0, cells - 1, t), :] + following)
     copies.append(out(fields - 1, P.at[slot]))
     copies[-1].start()
-    for n, k in enumerate(LATE):
-        P[n] = conserved[k]
+    def hydro(k, carry):
+        copy_in(k, k)
         for t in range(tiles):
             edge_l = jnp.where(local, sent_edge(R, 1, k, t), A[slots["mean_left"] + k])
             edge_r = jnp.where(local, sent_edge(R, 0, k, t), A[slots["mean_right"] + k])
@@ -566,9 +558,12 @@
                 [fix_polar(low, high, last, R[0, k, i, t], edge_r, t) for i in range(2)],
                 [H[k, layer(2, cell, t), :] for cell in ends])
             for cell, term in zip(ends, terms):
-                P[n, layer(0, cell, t), :] = P[n, layer(0, cell, t), :] + term
-        copies.append(out(k, P.at[n]))
-        copies[-1].start()
+                P[k, layer(0, cell, t), :] = P[k, layer(0, cell, t), :] + term
+        out(k, P.at[k]).start()
+        return carry
+
+    lax.fori_loop(0, nvar, hydro, 0)
+    copies += [out(k, P.at[k]) for k in range(nvar)]
     for c in copies:
         c.wait()
 
@@ -649,8 +644,8 @@
         ),
         in_specs=[near] * 6,
         out_specs=(far, far),
-        scratch_shapes=[shape(len(LATE) + 1, rows * ring, LANES), pltpu.SemaphoreType.DMA((fields + nface,))],
-        compiler_params=pltpu.CompilerParams(vmem_limit_bytes=4 * (len(LATE) + 1) * rows * ring * LANES + 2000000),
+        scratch_shapes=[shape(nvar + 1, rows * ring, LANES), pltpu.SemaphoreType.DMA((fields + nface,))],
+        compiler_params=pltpu.CompilerParams(vmem_limit_bytes=4 * (nvar + 1) * rows * ring * LANES + 2000000),
         name="spill",
     )(conserved, faces, *late)
     return unblocked(conserved, rows, cells, theta), unblocked(faces, rows, cells, theta)

time: 23.3 us -> 23.2 us (level)
  no operation moved by 1% of the time
where the time goes in v8:
time: 23.2 us; the launch traced here: 23.1 us
  Pallas kernels  22.4 us (97%)
  between operations  0.64 us (3%)
    pallas_call x1, Pallas kernels, body(): pl.pallas_call(functools.partial(kernel, nrow, nphi, rows, cells, tiles,...  19.8 us
    pallas_call x1, Pallas kernels, body(): pl.pallas_call(functools.partial(spill, nvar, rows, cells, tiles, cycles)...  2.59 us

profile of v8, /device:TPU:1, one launch (start us, length us, event | category | flops | bytes accessed | tf_op | source)
XLA Modules:
  0.0 23.1 jit_solution(12872786553204916611)
XLA Ops:
  0.6 19.8 %step.1 = (f32[8,1024,128]{2,1,0:T(8,128)S(1)}, f32[3,1024,128]{2,1,0:T(8,128)S(1)}, f32[23,32,128]{2,1,0:T(8,128)S(1)}, f32[5,1152,128]{2,1,0:T(8,128)S(1)}, f3...) custom-call(s32[16]{0:T(128)} %widths_far.1, f32[5,1024,128]{2,1,0:T(8,128)} %bitcast.20, ...), custom_call_target="tpu_custom_call" | custom-call | tf_op jit(solution)/shard_map/step/pallas_call | solution.py:596
  20.5 2.6 %spill.1 = (f32[8,1024,128]{2,1,0:T(8,128)}, f32[3,1024,128]{2,1,0:T(8,128)}) custom-call(f32[8,1024,128]{2,1,0:T(8,128)S(1)} %get-tuple-element.10.conserved, f32[3,1024,128]{2,1,0:T(8,128)S(1)} %get-tuple-element.11.faces, f32[23,32,128]{2,1,0:T(8,128)S(1)} %get-tuple-element.12.A, f32[5,1152,128]{2,1,0:T(8,128)S(1)} %get-tuple-element.13.H, ...), custom_call_target="tpu_custom_call" | custom-call | tf_op jit(solution)/shard_map/spill/pallas_call | solution.py:639
